TPU v7x, 128 devices: a whole 4x4x4 slice. The times are simulated.
128 devices in a mesh: seq: 32 (over y, z, core), batch: 4 (over x).
Axes of the slice: x: 4, y: 4, z: 4, core: 2. Of those that a mesh axis runs over, the one named last changes fastest.
Arguments:
- queries: bfloat16 [4, 4096, 4096], P('batch', 'seq'), may hold values from -130 to 130
- keys: bfloat16 [4, 4096, 1024], P('batch', 'seq'), may hold values from -4 to 4
- values: bfloat16 [4, 4096, 1024], P('batch', 'seq'), may hold values from -4 to 4
- lengths: int32 [4], P('batch'), may hold values from 2048 to 4096
- block_pos: int32 [4, 32], P('batch'), may hold values from 0 to 31, each once within a row
- w_in: bfloat16 [6144, 1024], replicated, may hold values from -0.078125 to 0.078125
- b_in: float32 [1024], replicated, may hold values from -3 to 3
- output_weight: bfloat16 [1024, 8], replicated, may hold values from -0.1875 to 0.1875
- output_bias: float32 [8], replicated, may hold values from 1 to 2
Outputs:
- grad_w_in: float32 [6144, 1024], P(('seq', 'batch'))
- grad_b_in: float32 [1024], replicated
- output_weight_gradient: float32 [1024, 8], replicated
- output_bias_gradient: float32 [8], replicated
Inputs may be any that keep to these rules, and one draw needn't show every extreme that they name: Each row of block_pos names every block 0 to 31 once.
All inputs are finite; a program needn't handle non-finite values.
Results may differ from a plain program's by a relative error of at most 0.0017.
The roundings to bfloat16 on the way count: a program that leaves them out, or rounds other values in their place, can miss the bound.
Values may be sent and summed in bfloat16 or wider, within the bound.
No kernel may reach another device: no remote copies, remote signals or barrier semaphores. Data moves between devices by JAX's collectives and lax.ppermute only.
A program may use at most 128 MiB of HBM per device.

v0:
```python
import math

import jax
import jax.numpy as jnp
from jax import lax
from jax.sharding import PartitionSpec as P


def split_up(array, dim, size):
    before, after = (array.shape[:dim], array.shape[dim + 1 :])
    return jnp.moveaxis(array.reshape(*before, size, -1, *after), dim, 0)


def sent_and_summed(array, axis, dim):
    size = lax.axis_size(axis)
    tiles = lax.all_to_all(split_up(array, dim, size), axis, 0, 0, tiled=True)
    return jnp.sum(tiles, axis=0)


def in_one(arrays, axis):
    ends = [0]
    for a in arrays:
        ends.append(ends[-1] + a.size)
    so_far = lax.psum(jnp.concatenate([a.ravel() for a in arrays]), axis)
    return tuple((so_far[b:e].reshape(a.shape) for a, b, e in zip(arrays, ends, ends[1:])))


def on_device(queries, keys, values, lengths, block_pos, w_in, b_in, output_weight, output_bias):
    q_rows = queries[0]
    k_rows = keys[0]
    v_rows = values[0]
    rows = q_rows.shape[0]
    heads_kv = output_weight.shape[1]
    head_size = k_rows.shape[1] // heads_kv
    group_index = q_rows.shape[1] // k_rows.shape[1]
    scale = 1.0 / math.sqrt(head_size)
    every_key = lax.all_gather(k_rows, "seq", axis=0, tiled=True)
    total = every_key.shape[0]
    order = block_pos[0]
    offsets = jnp.arange(rows, dtype=jnp.int32)
    key_pos = (order[:, None] * rows + offsets[None, :]).reshape(-1)
    mine = lax.axis_index("seq")
    query_pos = lax.dynamic_index_in_dim(order, mine, 0, keepdims=False) * rows + offsets
    limit = lengths[0]
    allowed = (key_pos[None, :] <= query_pos[:, None]) & (key_pos < limit)[None, :]
    query_live = (query_pos < limit).astype(jnp.float32)

    def group_mass(index, sums):
        q_part = lax.dynamic_slice_in_dim(
            q_rows, index * group_index * head_size, group_index * head_size, 1
        )
        q_part = q_part.reshape(rows, group_index, head_size)
        k_part = lax.dynamic_slice_in_dim(every_key, index * head_size, head_size, 1)
        scores = (
            jnp.einsum("qhd,kd->hqk", q_part, k_part, preferred_element_type=jnp.float32) * scale
        )
        masked = jnp.where(allowed[None], scores, -1e30)
        top = jnp.max(masked, axis=2, keepdims=True)
        weights = jnp.where(allowed[None], jnp.exp(masked - top), 0.0)
        denom = jnp.sum(weights, axis=2, keepdims=True)
        share = weights / denom * query_live[None, :, None]
        column = jnp.sum(share, axis=(0, 1))
        return lax.dynamic_update_index_in_dim(sums, column, index, 0)

    partial_value = lax.fori_loop(
        0, heads_kv, group_mass, jnp.zeros((heads_kv, total), jnp.float32)
    )
    mass = sent_and_summed(partial_value, "seq", 1)
    labels = jnp.log1p(mass).T
    features = jnp.concatenate([q_rows, k_rows, v_rows], axis=1)
    pre = jnp.dot(features, w_in, preferred_element_type=jnp.float32) + b_in
    act = jax.nn.silu(pre).astype(jnp.bfloat16)
    pred = jnp.dot(act, output_weight, preferred_element_type=jnp.float32) + output_bias
    norm = 1.0 / math.sqrt(lax.axis_size("batch") * total)
    resid = ((pred - labels) * query_live[:, None] * norm).astype(jnp.bfloat16)
    back = lax.dot_general(
        resid, output_weight, (((1,), (1,)), ((), ())), preferred_element_type=jnp.float32
    )
    sig = jax.nn.sigmoid(pre)
    delta = (back * sig * (1.0 + pre * (1.0 - sig))).astype(jnp.bfloat16)
    out_term = lax.dot_general(
        act, resid, (((0,), (0,)), ((), ())), preferred_element_type=jnp.float32
    )
    grad_b_in, output_weight_gradient, output_bias_gradient = in_one(
        (
            jnp.sum(delta.astype(jnp.float32), axis=0),
            out_term,
            jnp.sum(resid.astype(jnp.float32), axis=0),
        ),
        ("seq", "batch"),
    )
    grad_w_in = lax.psum_scatter(
        lax.dot_general(
            features, delta, (((0,), (0,)), ((), ())), preferred_element_type=jnp.float32
        ),
        ("seq", "batch"),
        scatter_dimension=0,
        tiled=True,
    )
    return (grad_w_in, grad_b_in, output_weight_gradient, output_bias_gradient)


def solution(mesh):
    return jax.shard_map(
        on_device,
        mesh=mesh,
        in_specs=(
            P("batch", "seq", None),
            P("batch", "seq", None),
            P("batch", "seq", None),
            P("batch"),
            P("batch", None),
            P(),
            P(),
            P(),
            P(),
        ),
        out_specs=(P(("seq", "batch"), None), P(), P(), P()),
        check_vma=False,
    )
```

profile of v0, /device:TPU:0, one launch (start us, length us, event | category | flops | bytes accessed | tf_op | source)
XLA Modules:
  0.0 518.8 jit_solution(12301234503528148574)
XLA Ops:
  15.2 50.5 %all-gather.3.cloned.1.call-done = bf16[1,4096,1024]{2,1,0:T(8,128)(2,1)} async-done(((bf16[1,128,1024]{2,1,0:T(8,128)(2,1)}), bf16[1,4096,1024]{2,1,0:T(8,128)(2,1)}) %all-gather.3.cloned.1.call-update) | async-done | bytes 8388624 | tf_op jit(solution)/shard_map/all_gather | solution.py:37
  65.7 170.6 %while.16 = (s32[]{:T(128)}, f32[8,4096]{1,0:T(8,128)}, bf16[4096,1024]{1,0:T(8,128)(2,1)}, bf16[128,4096]{0,1:T(8,128)(2,1)S(1)}, s32[128]{0:T(128)S(1)}, /*ind...) while((s32[]{:T(128)}, f32[8,4096]{1,0:T(8,128)}, ...), condition=%wide.region_4.5_spmd.clone, body=%wide.region_0.4_spmd.clone.sunk | while | flops 1097869184 | bytes 22091528 | solution.py:65
  68.4 8.6 %fusion.72 = f32[4,128,4096]{1,2,0:T(8,128)} fusion(pred[128,4096]{0,1:T(8,128)(4,1)S(1)} %compare_and_fusion.2, bf16[128,4,128]{0,2,1:T(8,128)(2,1)S(1)} %bitcast.69, bf16[4096,1024]{1,0:T(8,128)(2,1)} %get-tuple-element.300, s32[]{:T(128)S(6)} %select_n.79), kind=kOutput, calls=%fused_computation.2.clone.1 | convolution fusion | flops 545268736 | bytes 10616836 | tf_op jit(solution)/shard_map/while/body/eval_jaxpr/div | solution.py:61
  77.0 8.4 %multiply_reduce_fusion.2 = f32[4096]{0:T(1024)S(1)} fusion(f32[4,128,4096]{1,2,0:T(8,128)} %fusion.72, f32[128]{0:T(128)S(1)} %compare_convert_fusion.3, pred[128,4096]{0,1:T(8,128)(4,1)S(1)} %compare_and_fusion.2, bf16[128,4,128]{0,2,1:T(8,128)(2,1)S(1)} %bitcast.70, bf16[4096,1024]{1,0:T(8,128)(2,1)} %get-tuple-element.300, s32[]{:T(128)S(6)} %select_n.79), kind=kOutput, calls=%fused_computation.5.clone.1 | convolution fusion | flops 551551488 | bytes 10633732 | tf_op jit(solution)/shard_map/while/body/eval_jaxpr/sub | solution.py:59
  89.7 8.6 %fusion.72 = f32[4,128,4096]{1,2,0:T(8,128)} fusion(pred[128,4096]{0,1:T(8,128)(4,1)S(1)} %compare_and_fusion.2, bf16[128,4,128]{0,2,1:T(8,128)(2,1)S(1)} %bitcast.69, bf16[4096,1024]{1,0:T(8,128)(2,1)} %get-tuple-element.300, s32[]{:T(128)S(6)} %select_n.79), kind=kOutput, calls=%fused_computation.2.clone.1 | convolution fusion | flops 545268736 | bytes 10616836 | tf_op jit(solution)/shard_map/while/body/eval_jaxpr/div | solution.py:61
  98.3 8.4 %multiply_reduce_fusion.2 = f32[4096]{0:T(1024)S(1)} fusion(f32[4,128,4096]{1,2,0:T(8,128)} %fusion.72, f32[128]{0:T(128)S(1)} %compare_convert_fusion.3, pred[128,4096]{0,1:T(8,128)(4,1)S(1)} %compare_and_fusion.2, bf16[128,4,128]{0,2,1:T(8,128)(2,1)S(1)} %bitcast.70, bf16[4096,1024]{1,0:T(8,128)(2,1)} %get-tuple-element.300, s32[]{:T(128)S(6)} %select_n.79), kind=kOutput, calls=%fused_computation.5.clone.1 | convolution fusion | flops 551551488 | bytes 10633732 | tf_op jit(solution)/shard_map/while/body/eval_jaxpr/sub | solution.py:59
  111.0 8.6 %fusion.72 = f32[4,128,4096]{1,2,0:T(8,128)} fusion(pred[128,4096]{0,1:T(8,128)(4,1)S(1)} %compare_and_fusion.2, bf16[128,4,128]{0,2,1:T(8,128)(2,1)S(1)} %bitcast.69, bf16[4096,1024]{1,0:T(8,128)(2,1)} %get-tuple-element.300, s32[]{:T(128)S(6)} %select_n.79), kind=kOutput, calls=%fused_computation.2.clone.1 | convolution fusion | flops 545268736 | bytes 10616836 | tf_op jit(solution)/shard_map/while/body/eval_jaxpr/div | solution.py:61
  119.6 8.4 %multiply_reduce_fusion.2 = f32[4096]{0:T(1024)S(1)} fusion(f32[4,128,4096]{1,2,0:T(8,128)} %fusion.72, f32[128]{0:T(128)S(1)} %compare_convert_fusion.3, pred[128,4096]{0,1:T(8,128)(4,1)S(1)} %compare_and_fusion.2, bf16[128,4,128]{0,2,1:T(8,128)(2,1)S(1)} %bitcast.70, bf16[4096,1024]{1,0:T(8,128)(2,1)} %get-tuple-element.300, s32[]{:T(128)S(6)} %select_n.79), kind=kOutput, calls=%fused_computation.5.clone.1 | convolution fusion | flops 551551488 | bytes 10633732 | tf_op jit(solution)/shard_map/while/body/eval_jaxpr/sub | solution.py:59
  128.0 1.6 dynamic_update_slice.13
  132.4 8.6 %fusion.72 = f32[4,128,4096]{1,2,0:T(8,128)} fusion(pred[128,4096]{0,1:T(8,128)(4,1)S(1)} %compare_and_fusion.2, bf16[128,4,128]{0,2,1:T(8,128)(2,1)S(1)} %bitcast.69, bf16[4096,1024]{1,0:T(8,128)(2,1)} %get-tuple-element.300, s32[]{:T(128)S(6)} %select_n.79), kind=kOutput, calls=%fused_computation.2.clone.1 | convolution fusion | flops 545268736 | bytes 10616836 | tf_op jit(solution)/shard_map/while/body/eval_jaxpr/div | solution.py:61
  141.0 8.4 %multiply_reduce_fusion.2 = f32[4096]{0:T(1024)S(1)} fusion(f32[4,128,4096]{1,2,0:T(8,128)} %fusion.72, f32[128]{0:T(128)S(1)} %compare_convert_fusion.3, pred[128,4096]{0,1:T(8,128)(4,1)S(1)} %compare_and_fusion.2, bf16[128,4,128]{0,2,1:T(8,128)(2,1)S(1)} %bitcast.70, bf16[4096,1024]{1,0:T(8,128)(2,1)} %get-tuple-element.300, s32[]{:T(128)S(6)} %select_n.79), kind=kOutput, calls=%fused_computation.5.clone.1 | convolution fusion | flops 551551488 | bytes 10633732 | tf_op jit(solution)/shard_map/while/body/eval_jaxpr/sub | solution.py:59
  153.7 8.6 %fusion.72 = f32[4,128,4096]{1,2,0:T(8,128)} fusion(pred[128,4096]{0,1:T(8,128)(4,1)S(1)} %compare_and_fusion.2, bf16[128,4,128]{0,2,1:T(8,128)(2,1)S(1)} %bitcast.69, bf16[4096,1024]{1,0:T(8,128)(2,1)} %get-tuple-element.300, s32[]{:T(128)S(6)} %select_n.79), kind=kOutput, calls=%fused_computation.2.clone.1 | convolution fusion | flops 545268736 | bytes 10616836 | tf_op jit(solution)/shard_map/while/body/eval_jaxpr/div | solution.py:61
  162.3 8.4 %multiply_reduce_fusion.2 = f32[4096]{0:T(1024)S(1)} fusion(f32[4,128,4096]{1,2,0:T(8,128)} %fusion.72, f32[128]{0:T(128)S(1)} %compare_convert_fusion.3, pred[128,4096]{0,1:T(8,128)(4,1)S(1)} %compare_and_fusion.2, bf16[128,4,128]{0,2,1:T(8,128)(2,1)S(1)} %bitcast.70, bf16[4096,1024]{1,0:T(8,128)(2,1)} %get-tuple-element.300, s32[]{:T(128)S(6)} %select_n.79), kind=kOutput, calls=%fused_computation.5.clone.1 | convolution fusion | flops 551551488 | bytes 10633732 | tf_op jit(solution)/shard_map/while/body/eval_jaxpr/sub | solution.py:59
  175.0 8.6 %fusion.72 = f32[4,128,4096]{1,2,0:T(8,128)} fusion(pred[128,4096]{0,1:T(8,128)(4,1)S(1)} %compare_and_fusion.2, bf16[128,4,128]{0,2,1:T(8,128)(2,1)S(1)} %bitcast.69, bf16[4096,1024]{1,0:T(8,128)(2,1)} %get-tuple-element.300, s32[]{:T(128)S(6)} %select_n.79), kind=kOutput, calls=%fused_computation.2.clone.1 | convolution fusion | flops 545268736 | bytes 10616836 | tf_op jit(solution)/shard_map/while/body/eval_jaxpr/div | solution.py:61
  183.6 8.4 %multiply_reduce_fusion.2 = f32[4096]{0:T(1024)S(1)} fusion(f32[4,128,4096]{1,2,0:T(8,128)} %fusion.72, f32[128]{0:T(128)S(1)} %compare_convert_fusion.3, pred[128,4096]{0,1:T(8,128)(4,1)S(1)} %compare_and_fusion.2, bf16[128,4,128]{0,2,1:T(8,128)(2,1)S(1)} %bitcast.70, bf16[4096,1024]{1,0:T(8,128)(2,1)} %get-tuple-element.300, s32[]{:T(128)S(6)} %select_n.79), kind=kOutput, calls=%fused_computation.5.clone.1 | convolution fusion | flops 551551488 | bytes 10633732 | tf_op jit(solution)/shard_map/while/body/eval_jaxpr/sub | solution.py:59
  196.3 8.6 %fusion.72 = f32[4,128,4096]{1,2,0:T(8,128)} fusion(pred[128,4096]{0,1:T(8,128)(4,1)S(1)} %compare_and_fusion.2, bf16[128,4,128]{0,2,1:T(8,128)(2,1)S(1)} %bitcast.69, bf16[4096,1024]{1,0:T(8,128)(2,1)} %get-tuple-element.300, s32[]{:T(128)S(6)} %select_n.79), kind=kOutput, calls=%fused_computation.2.clone.1 | convolution fusion | flops 545268736 | bytes 10616836 | tf_op jit(solution)/shard_map/while/body/eval_jaxpr/div | solution.py:61
  204.9 8.4 %multiply_reduce_fusion.2 = f32[4096]{0:T(1024)S(1)} fusion(f32[4,128,4096]{1,2,0:T(8,128)} %fusion.72, f32[128]{0:T(128)S(1)} %compare_convert_fusion.3, pred[128,4096]{0,1:T(8,128)(4,1)S(1)} %compare_and_fusion.2, bf16[128,4,128]{0,2,1:T(8,128)(2,1)S(1)} %bitcast.70, bf16[4096,1024]{1,0:T(8,128)(2,1)} %get-tuple-element.300, s32[]{:T(128)S(6)} %select_n.79), kind=kOutput, calls=%fused_computation.5.clone.1 | convolution fusion | flops 551551488 | bytes 10633732 | tf_op jit(solution)/shard_map/while/body/eval_jaxpr/sub | solution.py:59
  217.6 8.6 %fusion.72 = f32[4,128,4096]{1,2,0:T(8,128)} fusion(pred[128,4096]{0,1:T(8,128)(4,1)S(1)} %compare_and_fusion.2, bf16[128,4,128]{0,2,1:T(8,128)(2,1)S(1)} %bitcast.69, bf16[4096,1024]{1,0:T(8,128)(2,1)} %get-tuple-element.300, s32[]{:T(128)S(6)} %select_n.79), kind=kOutput, calls=%fused_computation.2.clone.1 | convolution fusion | flops 545268736 | bytes 10616836 | tf_op jit(solution)/shard_map/while/body/eval_jaxpr/div | solution.py:61
  226.2 8.4 %multiply_reduce_fusion.2 = f32[4096]{0:T(1024)S(1)} fusion(f32[4,128,4096]{1,2,0:T(8,128)} %fusion.72, f32[128]{0:T(128)S(1)} %compare_convert_fusion.3, pred[128,4096]{0,1:T(8,128)(4,1)S(1)} %compare_and_fusion.2, bf16[128,4,128]{0,2,1:T(8,128)(2,1)S(1)} %bitcast.70, bf16[4096,1024]{1,0:T(8,128)(2,1)} %get-tuple-element.300, s32[]{:T(128)S(6)} %select_n.79), kind=kOutput, calls=%fused_computation.5.clone.1 | convolution fusion | flops 551551488 | bytes 10633732 | tf_op jit(solution)/shard_map/while/body/eval_jaxpr/sub | solution.py:59
  236.2 5.5 %all-to-all-start = ((f32[32,8,128]{2,1,0:T(8,128)}), f32[32,8,128]{2,1,0:T(8,128)S(1)}, u32[]{:S(2)}, u32[]{:S(2)}) async-start(f32[32,8,128]{2,1,0:T(8,128)} %bitcast.9), calls=%async_computation | async-start | bytes 262144 | tf_op jit(solution)/shard_map/all_to_all | solution.py:16
  242.0 6.5 %multiply_convert_fusion = (bf16[128,1024]{1,0:T(8,128)(2,1)S(1)}, f32[128,1024]{1,0:T(8,128)S(1)}) fusion(f32[1024]{0:T(1024)S(1)} %copy-done.1, bf16[6144,1024]{1,0:T(8,128)(2,1)} %param.16, bf16[128,1024]{0,1:T(8,128)(2,1)S(1)} %bitcast.73, bf16[128,1024]{0,1:T(8,128)(2,1)S(1)} %bitcast.71, bf16[128,4096]{0,1:T(8,128)(2,1)S(1)} %get-tuple-element.317), kind=kOutput, calls=%fused_computation.42 | convolution fusion | flops 1616117760 | bytes 14946304 | tf_op jit(solution)/shard_map/dot_general | solution.py:71
  250.3 13.2 %fusion.46 = f32[6144,1024]{1,0:T(8,128)} fusion(bf16[128,1024]{1,0:T(8,128)(2,1)S(1)} %get-tuple-element.212, bf16[128,1024]{0,1:T(8,128)(2,1)S(1)} %bitcast.74, bf16[128,1024]{0,1:T(8,128)(2,1)S(1)} %bitcast.72, bf16[128,4096]{0,1:T(8,128)(2,1)S(1)} %get-tuple-element.317), kind=kOutput, calls=%fused_computation.40 | convolution fusion | flops 1615331328 | bytes 27000832 | tf_op jit(solution)/shard_map/dot_general | solution.py:93
  264.1 67.0 %psum.7 = f32[9224]{0:T(1024)S(1)} all-reduce(f32[9224]{0:T(1024)S(1)} %pad_maximum_fusion.3), channel_id=1, replica_groups=mesh['seq'=32,'batch'=4] {'seq','batch'}, use_global_device_ids=true, to_apply=%region_9.10 | all-reduce | flops 9224 | bytes 73792 | tf_op jit(solution)/shard_map/psum | solution.py:24
  333.2 178.8 %reduce-scatter.2.cloned.1.call-done = f32[48,1024]{1,0:T(8,128)} async-done(((f32[6144,1024]{1,0:T(8,128)}), f32[48,1024]{1,0:T(8,128)}) %reduce-scatter.2.cloned.1.call-update) | async-done | bytes 196624 | tf_op jit(solution)/shard_map/reduce_scatter | solution.py:92
  (63 shorter events, 45.0 us)
Async XLA Ops:
  7.2 242.5 %copy-start = (bf16[1024,8]{0,1:T(8,128)(2,1)S(1)}, bf16[1024,8]{0,1:T(8,128)(2,1)}, u32[]{:S(2)}) copy-start(bf16[1024,8]{0,1:T(8,128)(2,1)} %param.18) | copy-start | bytes 49156
  7.2 58.5 %all-gather.3.cloned.1.call-start = ((), (), s32[]{:S(2)}) async-start(), calls=%async_computation.3 | async-start | bytes 8650752 | tf_op jit(solution)/shard_map/all_gather | solution.py:37
  65.7 176.3 %copy-start.1 = (f32[1024]{0:T(1024)S(1)}, f32[1024]{0:T(1024)}, u32[]{:S(2)}) copy-start(f32[1024]{0:T(1024)} %param.17) | copy-start | bytes 12292
  236.2 13.3 %all-to-all-start = ((f32[32,8,128]{2,1,0:T(8,128)}), f32[32,8,128]{2,1,0:T(8,128)S(1)}, u32[]{:S(2)}, u32[]{:S(2)}) async-start(f32[32,8,128]{2,1,0:T(8,128)} %bitcast.9), calls=%async_computation | async-start | bytes 262144 | tf_op jit(solution)/shard_map/all_to_all | solution.py:16
  241.7 270.2 %reduce-scatter.2.cloned.1.call-start = ((), (), s32[]{:S(2)}) async-start(), calls=%async_computation.2 | async-start | bytes 25362432 | tf_op jit(solution)/shard_map/reduce_scatter | solution.py:92
  242.0 7.6 %copy-start.2 = (f32[8]{0:T(128)S(1)}, f32[8]{0:T(128)}, u32[]{:S(2)}) copy-start(f32[8]{0:T(128)} %param.19) | copy-start | bytes 100
Sparse Core Ops, SparseCore 0:
  10.3 55.3 all-gather.2
  263.7 248.2 reduce-scatter.1
where the time goes:
time: 520 us; the launch traced here: 519 us
  waiting for transfers between devices  230 us (44%)
  matrix products  156 us (30%)
  blocking collectives  67 us (13%)
  other arithmetic  24.9 us (5%)
  local copies, waits for them, and re-layouts  19.4 us (4%)
  between operations  14.8 us (3%)
  starting transfers between devices  5.76 us (1%)
    reduce_scatter x1, waiting for transfers between devices, on_device(): lax.psum_scatter(lax.dot_general(features, delta, (((0,), (0,)), ((), ())...  179 us
    div x8, matrix products, group_mass(): share = weights / denom * query_live[None, :, None]  68.8 us
    sub x8, matrix products, group_mass(): weights = jnp.where(allowed[None], jnp.exp(masked - top), 0.0)  67 us
    psum x1, blocking collectives, in_one(): so_far = lax.psum(jnp.concatenate([a.ravel() for a in arrays]), axis)  67 us
    all_gather x1, waiting for transfers between devices, on_device(): every_key = lax.all_gather(k_rows, 'seq', axis=0, tiled=True)  50.5 us
    dot_general x1, matrix products, on_device(): lax.dot_general(features, delta, (((0,), (0,)), ((), ())), preferred_elem...  13.2 us
    dynamic_update_slice x8, local copies, waits for them, and re-layouts, group_mass(): return lax.dynamic_update_index_in_dim(sums, column, index, 0)  12.9 us
    and x8, other arithmetic, on_device(): (key_pos[None, :] <= query_pos[:, None]) & (key_pos < limit)[None, :]  11.1 us
  transfers between devices with their start and end apart: 3, of which 3 were waited for; matrix products, arithmetic and copies ran while one was open for 3% of the time, Pallas kernels for 0%

commit v1 on v0

v1 whole, which is shorter than its diff:
```python
import functools
import math

import jax
import jax.numpy as jnp
from jax import lax
from jax.experimental import pallas as pl
from jax.experimental.pallas import tpu as pltpu
from jax.sharding import PartitionSpec as P

BLOCK = 128
CHUNK = 256


def mass_kernel(order_ref, where_ref, limit_ref, q_ref, k_ref, out_ref, keys, scores, col, high, *, scale):
    blocks = q_ref.shape[0] // BLOCK
    per = CHUNK // BLOCK
    limit = limit_ref[0]
    factor = scale * math.log2(math.e)

    def by_position(p, carry):
        start = pl.multiple_of(where_ref[p] * BLOCK, BLOCK)
        keys[pl.ds(pl.multiple_of(p * BLOCK, BLOCK), BLOCK), :] = k_ref[pl.ds(start, BLOCK), :]
        return carry

    lax.fori_loop(0, blocks, by_position, 0)
    col[...] = jnp.zeros_like(col)
    row = lax.broadcasted_iota(jnp.int32, (CHUNK, CHUNK), 0)
    column = lax.broadcasted_iota(jnp.int32, (CHUNK, CHUNK), 1)

    def folded(tile, op):
        out = tile[:, :BLOCK]
        for i in range(1, per):
            out = op(out, tile[:, i * BLOCK : (i + 1) * BLOCK])
        return out

    def row_block(r, carry):
        parts = [
            q_ref[pl.ds(pl.multiple_of(where_ref[r * per + i] * BLOCK, BLOCK), BLOCK), :] for i in range(per)
        ]
        q_rows = jnp.concatenate(parts, axis=0)

        def product(c):
            k_rows = keys[pl.ds(pl.multiple_of(c * CHUNK, CHUNK), CHUNK), :]
            return lax.dot_general(
                q_rows, k_rows, (((1,), (1,)), ((), ())), preferred_element_type=jnp.float32
            )

        own = jnp.where((column <= row) & (column + r * CHUNK < limit), product(r), -1e30)
        scores[r] = own
        high[...] = folded(own, jnp.maximum)

        def score_step(c, carry):
            tile = product(c)
            scores[c] = tile
            high[...] = jnp.maximum(high[...], folded(tile, jnp.maximum))
            return carry

        lax.fori_loop(0, r, score_step, 0)
        top = jnp.max(high[...], axis=1, keepdims=True)
        high[...] = jnp.zeros_like(high)

        def exp_step(c, carry):
            tile = jnp.exp2((scores[c] - top) * factor)
            scores[c] = tile
            high[...] += folded(tile, jnp.add)
            return carry

        lax.fori_loop(0, r + 1, exp_step, 0)
        total = jnp.sum(high[...], axis=1, keepdims=True)
        live = lax.broadcasted_iota(jnp.int32, (CHUNK, 1), 0) + r * CHUNK < limit
        weight = jnp.where(live, 1.0 / total, 0.0)

        def column_step(c, carry):
            tile = scores[c] * weight
            part = jnp.sum(tile.reshape(CHUNK // 8, 8, CHUNK), axis=0)
            for i in range(per):
                col[c * per + i] += part[:, i * BLOCK : (i + 1) * BLOCK]
            return carry

        lax.fori_loop(0, r + 1, column_step, 0)
        return carry

    lax.fori_loop(0, (limit + CHUNK - 1) // CHUNK, row_block, 0)

    def store(i, carry):
        out_ref[i] = col[order_ref[i]]
        return carry

    lax.fori_loop(0, blocks, store, 0)


def head_mass(order, where, limit, q_rows, k_rows, scale):
    tokens, size = q_rows.shape
    blocks = tokens // BLOCK
    smem = pl.BlockSpec(memory_space=pltpu.SMEM)
    vmem = pl.BlockSpec(memory_space=pltpu.VMEM)
    return pl.pallas_call(
        functools.partial(mass_kernel, scale=scale),
        out_shape=jax.ShapeDtypeStruct((blocks, 8, BLOCK), jnp.float32),
        in_specs=[smem, smem, smem, vmem, vmem],
        out_specs=vmem,
        scratch_shapes=[
            pltpu.VMEM((tokens, size), jnp.bfloat16),
            pltpu.VMEM((tokens // CHUNK, CHUNK, CHUNK), jnp.float32),
            pltpu.VMEM((blocks, 8, BLOCK), jnp.float32),
            pltpu.VMEM((CHUNK, BLOCK), jnp.float32),
        ],
        compiler_params=pltpu.CompilerParams(vmem_limit_bytes=24 * 1024 * 1024),
        cost_estimate=pl.CostEstimate(
            flops=2 * tokens * tokens * size, bytes_accessed=4 * tokens * size, transcendentals=tokens * tokens // 2
        ),
        name="head_mass",
    )(order, where, limit, q_rows, k_rows)


def exchanged(array, axis):
    return lax.all_to_all(array, axis, 0, 0, tiled=True)


def on_device(queries, keys, values, lengths, block_pos, w_in, b_in, output_weight, output_bias):
    q_rows = queries[0]
    k_rows = keys[0]
    v_rows = values[0]
    rows = q_rows.shape[0]
    seq = lax.axis_size("seq")
    batch = lax.axis_size("batch")
    heads_kv = output_weight.shape[1]
    hidden = output_weight.shape[0]
    head_size = k_rows.shape[1] // heads_kv
    group = q_rows.shape[1] // k_rows.shape[1]
    heads = heads_kv * group
    total = rows * seq
    order = block_pos[0]
    offsets = jnp.arange(rows, dtype=jnp.int32)
    mine = lax.axis_index("seq")
    query_pos = lax.dynamic_index_in_dim(order, mine, 0, keepdims=False) * rows + offsets
    limit = lengths[0]
    query_live = (query_pos < limit).astype(jnp.float32)
    where = jnp.sum(
        jnp.where(order[None, :] == jnp.arange(seq, dtype=jnp.int32)[:, None], jnp.arange(seq, dtype=jnp.int32)[None, :], 0),
        axis=1,
    ).astype(jnp.int32)

    by_head = jnp.moveaxis(q_rows.reshape(rows, heads, head_size), 1, 0)
    keys_by_head = jnp.moveaxis(k_rows.reshape(rows, heads_kv, head_size), 1, 0)
    keys_by_head = jnp.broadcast_to(keys_by_head[:, None], (heads_kv, group, rows, head_size)).reshape(
        heads, rows, head_size
    )
    both = exchanged(jnp.stack([by_head, keys_by_head], axis=1), "seq")
    own_q = both[:, 0].reshape(total, head_size)
    own_k = both[:, 1].reshape(total, head_size)
    partial = head_mass(order, where, lengths, own_q, own_k, 1.0 / math.sqrt(head_size))

    features = jnp.concatenate([q_rows, k_rows, v_rows], axis=1)
    width = features.shape[1] // seq
    spread = exchanged(jnp.moveaxis(features.reshape(rows, seq, width), 1, 0), "seq").reshape(total, width)

    pre = jnp.dot(features, w_in, preferred_element_type=jnp.float32) + b_in
    act = jax.nn.silu(pre).astype(jnp.bfloat16)
    pred = jnp.dot(act, output_weight, preferred_element_type=jnp.float32) + output_bias

    arrived = exchanged(partial, "seq")
    mass = jnp.sum(arrived.reshape(heads_kv, group * 8, rows), axis=1)
    labels = jnp.log1p(mass).T
    norm = 1.0 / math.sqrt(batch * total)
    resid = ((pred - labels) * query_live[:, None] * norm).astype(jnp.bfloat16)
    back = lax.dot_general(
        resid, output_weight, (((1,), (1,)), ((), ())), preferred_element_type=jnp.float32
    )
    sig = jax.nn.sigmoid(pre)
    delta = (back * sig * (1.0 + pre * (1.0 - sig))).astype(jnp.bfloat16)
    out_term = lax.dot_general(
        act, resid, (((0,), (0,)), ((), ())), preferred_element_type=jnp.float32
    )
    small = jnp.concatenate(
        [
            jnp.sum(delta.astype(jnp.float32), axis=0),
            out_term.ravel(),
            jnp.sum(resid.astype(jnp.float32), axis=0),
        ]
    )
    size = small.shape[0]
    piece = -(-size // (seq * 128)) * 128
    small = jnp.pad(small, (0, seq * piece - size)).reshape(seq, piece)
    small = jnp.sum(exchanged(small, "seq"), axis=0)
    small = exchanged(jnp.broadcast_to(small[None], (seq * batch, piece)), ("seq", "batch"))
    small = jnp.sum(small.reshape(seq, batch, piece), axis=1).ravel()
    grad_b_in = small[:hidden]
    output_weight_gradient = small[hidden : hidden + hidden * heads_kv].reshape(hidden, heads_kv)
    output_bias_gradient = small[hidden + hidden * heads_kv : size]

    every_delta = lax.all_gather(delta, "seq", axis=0, tiled=True)
    block = lax.dot_general(
        spread, every_delta, (((0,), (0,)), ((), ())), preferred_element_type=jnp.float32
    )
    block = block.reshape(batch, width // batch, hidden)
    grad_w_in = jnp.sum(exchanged(block, "batch"), axis=0)
    return (grad_w_in, grad_b_in, output_weight_gradient, output_bias_gradient)


def solution(mesh):
    return jax.shard_map(
        on_device,
        mesh=mesh,
        in_specs=(
            P("batch", "seq", None),
            P("batch", "seq", None),
            P("batch", "seq", None),
            P("batch"),
            P("batch", None),
            P(),
            P(),
            P(),
            P(),
        ),
        out_specs=(P(("seq", "batch"), None), P(), P(), P()),
        check_vma=False,
    )
```

time: 520 us -> 204 us (0.39)
  waiting for transfers between devices: 230 us -> 74.5 us
  matrix products: 156 us -> 14.7 us
  blocking collectives: 67 us -> 0 us
  starting transfers between devices: 5.76 us -> 64.9 us
  other arithmetic: 24.9 us -> 4.92 us
  Pallas kernels: 0 us -> 16.3 us
  local copies, waits for them, and re-layouts: 19.4 us -> 13.9 us
    reduce_scatter x1 -> x0, waiting for transfers between devices: 179 us -> none  [on_device(): lax.psum_scatter(lax.dot_general(features, delta, (((0,), (0,)), ((), ())...]
    div x8 -> x0, matrix products: 68.8 us -> none  [group_mass(): share = weights / denom * query_live[None, :, None]]
    sub x8 -> x0, matrix products: 67 us -> none  [group_mass(): weights = jnp.where(allowed[None], jnp.exp(masked - top), 0.0)]
    psum x1 -> x0, blocking collectives: 67 us -> none  [in_one(): so_far = lax.psum(jnp.concatenate([a.ravel() for a in arrays]), axis)]
    all_to_all x1 -> x6, waiting for transfers between devices: 0.43 us -> 62.7 us  [exchanged(): return lax.all_to_all(array, axis, 0, 0, tiled=True)]
    all_to_all x1 -> x6, starting transfers between devices: 5.5 us -> 64.9 us  [exchanged(): return lax.all_to_all(array, axis, 0, 0, tiled=True)]
    all_gather x1, waiting for transfers between devices: 50.5 us -> 11.7 us  [on_device(): every_delta = lax.all_gather(delta, 'seq', axis=0, tiled=True)]
    pallas_call x0 -> x1, Pallas kernels: none -> 16.3 us  [head_mass(): pl.pallas_call(functools.partial(mass_kernel, scale=scale), out_shape=jax...]
  transfers between devices with their start and end apart: 3 -> 7, of which waited for: 3 -> 5; matrix products, arithmetic and copies ran while one was open for 3% -> 12% of each run, Pallas kernels for 0% -> 0%
where the time goes in v1:
time: 204 us
  waiting for transfers between devices  74.5 us (37%)
  starting transfers between devices  64.9 us (32%)
  Pallas kernels  16.3 us (8%)
  between operations  14.9 us (7%)
  matrix products  14.7 us (7%)
  local copies, waits for them, and re-layouts  13.9 us (7%)
  other arithmetic  4.92 us (2%)
    all_to_all x6, starting transfers between devices, exchanged(): return lax.all_to_all(array, axis, 0, 0, tiled=True)  64.9 us
    all_to_all x6, waiting for transfers between devices, exchanged(): return lax.all_to_all(array, axis, 0, 0, tiled=True)  62.7 us
    pallas_call x1, Pallas kernels, head_mass(): pl.pallas_call(functools.partial(mass_kernel, scale=scale), out_shape=jax...  16.3 us
    all_gather x1, waiting for transfers between devices, on_device(): every_delta = lax.all_gather(delta, 'seq', axis=0, tiled=True)  11.7 us
    dot_general x1, matrix products, on_device(): lax.dot_general(spread, every_delta, (((0,), (0,)), ((), ())), preferred_...  6.55 us
    dot_general x1, matrix products, on_device(): pre = jnp.dot(features, w_in, preferred_element_type=jnp.float32) + b_in  6.52 us
    unnamed x15, local copies, waits for them, and re-layouts  6.36 us
  transfers between devices with their start and end apart: 7, of which 5 were waited for; matrix products, arithmetic and copies ran while one was open for 12% of the time, Pallas kernels for 0%

profile of v1, /device:TPU:0, one launch (start us, length us, event | category | flops | bytes accessed | tf_op | source)
XLA Modules:
  0.0 204.1 jit_solution(9531167716676986366)
XLA Ops:
  7.2 1.0 copy.85
  8.4 1.6 copy.67
  10.5 2.8 %copy.73 = bf16[32,2,128,128]{3,2,1,0:T(8,128)(2,1)} copy(bf16[32,2,128,128]{2,3,0,1:T(8,128)(2,1)S(1)} %pad_maximum_fusion) | data formatting | bytes 4194304 | tf_op jit(solution)/shard_map/stack | solution.py:150
  13.2 8.6 %all-to-all-start.1 = ((bf16[32,2,128,128]{3,2,1,0:T(8,128)(2,1)}), bf16[32,2,128,128]{3,2,1,0:T(8,128)(2,1)S(1)}, u32[]{:S(2)}, u32[]{:S(2)}) async-start(bf16[32,2,128,128]{3,2,1,0:T(8,128)(2,1)} %copy.73), calls=%async_computation.1 | async-start | bytes 4194304 | tf_op jit(solution)/shard_map/all_to_all | solution.py:118
  21.8 1.1 copy.68
  23.6 1.8 copy.69
  25.5 25.2 %all-to-all-done.1 = bf16[32,2,128,128]{3,2,1,0:T(8,128)(2,1)S(1)} async-done(((bf16[32,2,128,128]{3,2,1,0:T(8,128)(2,1)}), bf16[32,2,128,128]{3,2,1,0:T(8,128)(2,1)S(1)}, u32[]{:S(2)}, u32[]{:S(2)}) %all-to-all-start.1) | async-done | bytes 2097184 | tf_op jit(solution)/shard_map/all_to_all | solution.py:118
  50.9 16.3 %head_mass.1 = f32[32,8,128]{2,1,0:T(8,128)} custom-call(s32[32]{0:T(128)S(1)} %bitcast.49, s32[32]{0:T(128)S(1)} %select_reduce_fusion.where_ref, s32[1]{0:T(128)} %copy.87.limit_ref, bf16[4096,128]{1,0:T(8,128)(2,1)S(1)} %bitcast.47, bf16[4096,128]{1,0:T(8,128)(2,1)S(1)} %bitcast.46), custom_call_target="tpu_custom_call" | custom-call | flops 4294967296 | bytes 2097152 | tf_op jit(solution)/shard_map/head_mass/pallas_call | solution.py:98
  67.2 3.9 %all-to-all-start.2 = ((f32[32,8,128]{2,1,0:T(8,128)}), f32[32,8,128]{2,1,0:T(8,128)S(1)}, u32[]{:S(2)}, u32[]{:S(2)}) async-start(f32[32,8,128]{2,1,0:T(8,128)} %head_mass.1), calls=%async_computation.2 | async-start | bytes 262144 | tf_op jit(solution)/shard_map/all_to_all | solution.py:118
  71.1 6.5 %multiply_convert_fusion = (bf16[128,1024]{1,0:T(8,128)(2,1)S(1)}, f32[128,1024]{1,0:T(8,128)S(1)}) fusion(f32[1024]{0:T(1024)S(1)} %copy-done.3, bf16[6144,1024]{1,0:T(8,128)(2,1)} %param.14, bf16[128,1024]{0,1:T(8,128)(2,1)S(1)} %bitcast.58, bf16[128,1024]{0,1:T(8,128)(2,1)S(1)} %bitcast.56, bf16[128,4096]{0,1:T(8,128)(2,1)S(1)} %bitcast.51), kind=kOutput, calls=%fused_computation.15 | convolution fusion | flops 1616117760 | bytes 14946304 | tf_op jit(solution)/shard_map/dot_general | solution.py:159
  79.3 1.1 convert_reduce_fusion
  80.4 1.3 pad_maximum_fusion.1
  81.7 7.4 %all-to-all-start = ((bf16[32,128,192]{1,2,0:T(8,128)(2,1)}), bf16[32,128,192]{1,2,0:T(8,128)(2,1)S(1)}, u32[]{:S(2)}, u32[]{:S(2)}) async-start(bf16[32,128,192]{1,2,0:T(8,128)(2,1)} %bitcast.53), calls=%async_computation | async-start | bytes 3145728 | tf_op jit(solution)/shard_map/all_to_all | solution.py:118
  90.3 21.8 %all-to-all-done = bf16[32,128,192]{1,2,0:T(8,128)(2,1)S(1)} async-done(((bf16[32,128,192]{1,2,0:T(8,128)(2,1)}), bf16[32,128,192]{1,2,0:T(8,128)(2,1)S(1)}, u32[]{:S(2)}, u32[]{:S(2)}) %all-to-all-start) | async-done | bytes 1572896 | tf_op jit(solution)/shard_map/all_to_all | solution.py:118
  112.1 3.9 %all-to-all-start.4 = ((f32[32,1,384]{2,1,0:T(1,128)}), f32[32,1,384]{2,1,0:T(1,128)S(1)}, u32[]{:S(2)}, u32[]{:S(2)}) async-start(f32[32,1,384]{2,1,0:T(1,128)} %bitcast.20), calls=%async_computation.4 | async-start | bytes 98304 | tf_op jit(solution)/shard_map/all_to_all | solution.py:118
  116.0 1.5 copy_bitcast_fusion
  117.4 6.0 %all-to-all-done.4 = f32[32,1,384]{2,1,0:T(1,128)S(1)} async-done(((f32[32,1,384]{2,1,0:T(1,128)}), f32[32,1,384]{2,1,0:T(1,128)S(1)}, u32[]{:S(2)}, u32[]{:S(2)}) %all-to-all-start.4) | async-done | bytes 49184 | tf_op jit(solution)/shard_map/all_to_all | solution.py:118
  123.5 0.8 broadcast_in_dim.19
  124.3 36.9 %all-to-all-start.5 = ((f32[128,1,384]{2,1,0:T(1,128)}), f32[128,1,384]{2,1,0:T(1,128)S(1)}, u32[]{:S(2)}, u32[]{:S(2)}) async-start(f32[128,1,384]{2,1,0:T(1,128)} %broadcast_in_dim.19), calls=%async_computation.5 | async-start | bytes 393216 | tf_op jit(solution)/shard_map/all_to_all | solution.py:118
  161.2 11.7 %all-gather.2.cloned.1.call-done = bf16[4096,1024]{1,0:T(8,128)(2,1)} async-done(((bf16[128,1024]{1,0:T(8,128)(2,1)}), bf16[4096,1024]{1,0:T(8,128)(2,1)}) %all-gather.2.cloned.1.call-update) | async-done | bytes 8388624 | tf_op jit(solution)/shard_map/all_gather | solution.py:193
  172.9 6.6 %fusion = f32[4,48,1024]{2,1,0:T(8,128)} fusion(bf16[4,48,4096]{2,1,0:T(8,128)(2,1)} %bitcast.55, bf16[4096,1024]{1,0:T(8,128)(2,1)} %all-gather.2.cloned.1.call-done), kind=kOutput, calls=%fused_computation | convolution fusion | flops 1610612736 | bytes 10747904 | tf_op jit(solution)/shard_map/dot_general | solution.py:194
  179.5 4.3 %all-to-all-start.3 = ((f32[4,48,1024]{2,1,0:T(8,128)}), f32[4,48,1024]{2,1,0:T(8,128)S(1)}, u32[]{:S(2)}, u32[]{:S(2)}) async-start(f32[4,48,1024]{2,1,0:T(8,128)} %fusion), calls=%async_computation.3 | async-start | bytes 1572864 | tf_op jit(solution)/shard_map/all_to_all | solution.py:118
  186.0 0.8 copy.78
  186.8 9.7 %all-to-all-done.3 = f32[4,48,1024]{2,1,0:T(8,128)S(1)} async-done(((f32[4,48,1024]{2,1,0:T(8,128)}), f32[4,48,1024]{2,1,0:T(8,128)S(1)}, u32[]{:S(2)}, u32[]{:S(2)}) %all-to-all-start.3) | async-done | bytes 786464 | tf_op jit(solution)/shard_map/all_to_all | solution.py:118
  (37 shorter events, 6.7 us)
Async XLA Ops:
  7.2 71.8 %copy-start = (bf16[1024,8]{0,1:T(8,128)(2,1)S(1)}, bf16[1024,8]{0,1:T(8,128)(2,1)}, u32[]{:S(2)}) copy-start(bf16[1024,8]{0,1:T(8,128)(2,1)} %param.16) | copy-start | bytes 49156
  13.2 12.2 %copy-start.1 = (s32[1,32]{1,0:T(1,128)S(1)}, s32[1,32]{1,0:T(1,128)}, u32[]{:S(2)}) copy-start(s32[1,32]{1,0:T(1,128)} %param.13) | copy-start | bytes 388
  13.2 37.5 %all-to-all-start.1 = ((bf16[32,2,128,128]{3,2,1,0:T(8,128)(2,1)}), bf16[32,2,128,128]{3,2,1,0:T(8,128)(2,1)S(1)}, u32[]{:S(2)}, u32[]{:S(2)}) async-start(bf16[32,2,128,128]{3,2,1,0:T(8,128)(2,1)} %copy.73), calls=%async_computation.1 | async-start | bytes 4194304 | tf_op jit(solution)/shard_map/all_to_all | solution.py:118
  50.9 20.2 %copy-start.2 = (bf16[1,128,1024]{1,2,0:T(8,128)(2,1)S(1)}, bf16[1,128,1024]{1,2,0:T(8,128)(2,1)}, u32[]{:S(2)}) copy-start(bf16[1,128,1024]{1,2,0:T(8,128)(2,1)} %copy.69) | copy-start | bytes 786436
  50.9 20.2 %copy-start.3 = (f32[1024]{0:T(1024)S(1)}, f32[1024]{0:T(1024)}, u32[]{:S(2)}) copy-start(f32[1024]{0:T(1024)} %param.15) | copy-start | bytes 12292
  67.2 11.7 %all-to-all-start.2 = ((f32[32,8,128]{2,1,0:T(8,128)}), f32[32,8,128]{2,1,0:T(8,128)S(1)}, u32[]{:S(2)}, u32[]{:S(2)}) async-start(f32[32,8,128]{2,1,0:T(8,128)} %head_mass.1), calls=%async_computation.2 | async-start | bytes 262144 | tf_op jit(solution)/shard_map/all_to_all | solution.py:118
  71.1 101.8 %all-gather.2.cloned.1.call-start = ((), (), s32[]{:S(2)}) async-start(), calls=%async_computation.6 | async-start | bytes 8650752 | tf_op jit(solution)/shard_map/all_gather | solution.py:193
  71.1 7.9 %copy-start.4 = (f32[8]{0:T(128)S(1)}, f32[8]{0:T(128)}, u32[]{:S(2)}) copy-start(f32[8]{0:T(128)} %param.17) | copy-start | bytes 100
  81.7 30.4 %all-to-all-start = ((bf16[32,128,192]{1,2,0:T(8,128)(2,1)}), bf16[32,128,192]{1,2,0:T(8,128)(2,1)S(1)}, u32[]{:S(2)}, u32[]{:S(2)}) async-start(bf16[32,128,192]{1,2,0:T(8,128)(2,1)} %bitcast.53), calls=%async_computation | async-start | bytes 3145728 | tf_op jit(solution)/shard_map/all_to_all | solution.py:118
  112.1 11.3 %all-to-all-start.4 = ((f32[32,1,384]{2,1,0:T(1,128)}), f32[32,1,384]{2,1,0:T(1,128)S(1)}, u32[]{:S(2)}, u32[]{:S(2)}) async-start(f32[32,1,384]{2,1,0:T(1,128)} %bitcast.20), calls=%async_computation.4 | async-start | bytes 98304 | tf_op jit(solution)/shard_map/all_to_all | solution.py:118
  124.3 55.2 %all-to-all-start.5 = ((f32[128,1,384]{2,1,0:T(1,128)}), f32[128,1,384]{2,1,0:T(1,128)S(1)}, u32[]{:S(2)}, u32[]{:S(2)}) async-start(f32[128,1,384]{2,1,0:T(1,128)} %broadcast_in_dim.19), calls=%async_computation.5 | async-start | bytes 393216 | tf_op jit(solution)/shard_map/all_to_all | solution.py:118
  179.5 17.0 %all-to-all-start.3 = ((f32[4,48,1024]{2,1,0:T(8,128)}), f32[4,48,1024]{2,1,0:T(8,128)S(1)}, u32[]{:S(2)}, u32[]{:S(2)}) async-start(f32[4,48,1024]{2,1,0:T(8,128)} %fusion), calls=%async_computation.3 | async-start | bytes 1572864 | tf_op jit(solution)/shard_map/all_to_all | solution.py:118
Sparse Core Ops, SparseCore 0:
  80.5 92.3 all-gather.1

commit v2 on v1

v2 whole, which is shorter than its diff:
```python
import functools
import math

import jax
import jax.numpy as jnp
from jax import lax
from jax.experimental import pallas as pl
from jax.experimental.pallas import tpu as pltpu
from jax.sharding import Mesh
from jax.sharding import PartitionSpec as P

BLOCK = 128
QUERIES = 512
KEYS = 512


def mass_kernel(order_ref, where_ref, limit_ref, q_ref, k_ref, out_ref, keys, scores, col, *, scale):
    blocks = q_ref.shape[0] // BLOCK
    limit = limit_ref[0]
    factor = scale * math.log2(math.e)
    diagonal = QUERIES // KEYS
    lanes = QUERIES // BLOCK

    def by_position(p, carry):
        start = pl.multiple_of(where_ref[p] * BLOCK, BLOCK)
        keys[pl.ds(pl.multiple_of(p * BLOCK, BLOCK), BLOCK), :] = k_ref[pl.ds(start, BLOCK), :]
        return carry

    lax.fori_loop(0, blocks, by_position, 0)
    col[...] = jnp.zeros_like(col)
    key = lax.broadcasted_iota(jnp.int32, (KEYS, QUERIES), 0)
    query = lax.broadcasted_iota(jnp.int32, (KEYS, QUERIES), 1)

    def folded(tile, op):
        return op(tile.reshape(KEYS // 8, 8, QUERIES), axis=0)

    def column_step(c, slot, weight):
        tile = scores[slot, c] * weight
        part = tile[:, :BLOCK]
        for i in range(1, lanes):
            part = part + tile[:, i * BLOCK : (i + 1) * BLOCK]
        col[c] += part

    def query_block(r, weight):
        parts = [
            q_ref[pl.ds(pl.multiple_of(where_ref[r * lanes + i] * BLOCK, BLOCK), BLOCK), :] for i in range(lanes)
        ]
        q_rows = jnp.concatenate(parts, axis=0)
        slot = lax.rem(r, 2)

        def product(c):
            k_rows = keys[pl.ds(pl.multiple_of(c * KEYS, KEYS), KEYS), :]
            return (
                lax.dot_general(k_rows, q_rows, (((1,), (1,)), ((), ())), preferred_element_type=jnp.float32)
                * factor
            )

        high = jnp.full((8, QUERIES), -1e30, jnp.float32)
        for d in range(diagonal):
            c = r * diagonal + d
            allowed = (key + d * KEYS <= query) & (key + c * KEYS < limit)
            tile = jnp.where(allowed, product(c), -1e30)
            scores[slot, c] = tile
            high = jnp.maximum(high, folded(tile, jnp.max))

        def score_step(c, high):
            tile = product(c)
            scores[slot, c] = tile
            column_step(c, 1 - slot, weight)
            return jnp.maximum(high, folded(tile, jnp.max))

        high = lax.fori_loop(0, r * diagonal, score_step, high)
        top = jnp.max(high, axis=0, keepdims=True)

        def exp_step(c, sums):
            tile = jnp.exp2(scores[slot, c] - top)
            scores[slot, c] = tile
            return sums + folded(tile, jnp.sum)

        sums = lax.fori_loop(0, (r + 1) * diagonal, exp_step, jnp.zeros((8, QUERIES), jnp.float32))
        total = jnp.sum(sums, axis=0, keepdims=True)
        live = lax.broadcasted_iota(jnp.int32, (1, QUERIES), 1) + r * QUERIES < limit
        return jnp.where(live, 1.0 / total, 0.0)

    count = (limit + QUERIES - 1) // QUERIES
    weight = lax.fori_loop(0, count, query_block, jnp.zeros((1, QUERIES), jnp.float32))
    last = lax.rem(count - 1, 2)

    def last_step(c, carry):
        column_step(c, last, weight)
        return carry

    lax.fori_loop(0, count * diagonal, last_step, 0)

    def store(i, carry):
        p = order_ref[i]
        per = KEYS // BLOCK
        own = col[p // per, pl.ds(pl.multiple_of(lax.rem(p, per) * BLOCK, BLOCK), BLOCK), :]
        out_ref[pl.ds(i, 1), :] = jnp.sum(own.T, axis=0, keepdims=True)
        return carry

    lax.fori_loop(0, blocks, store, 0)


def head_mass(order, where, limit, q_rows, k_rows, scale):
    tokens, size = q_rows.shape
    smem = pl.BlockSpec(memory_space=pltpu.SMEM)
    vmem = pl.BlockSpec(memory_space=pltpu.VMEM)
    return pl.pallas_call(
        functools.partial(mass_kernel, scale=scale),
        out_shape=jax.ShapeDtypeStruct((tokens // BLOCK, BLOCK), jnp.float32),
        in_specs=[smem, smem, smem, vmem, vmem],
        out_specs=vmem,
        scratch_shapes=[
            pltpu.VMEM((tokens, size), jnp.bfloat16),
            pltpu.VMEM((2, tokens // KEYS, KEYS, QUERIES), jnp.float32),
            pltpu.VMEM((tokens // KEYS, KEYS, BLOCK), jnp.float32),
        ],
        compiler_params=pltpu.CompilerParams(vmem_limit_bytes=48 * 1024 * 1024),
        cost_estimate=pl.CostEstimate(
            flops=2 * tokens * tokens * size, bytes_accessed=4 * tokens * size, transcendentals=tokens * tokens // 2
        ),
        name="head_mass",
    )(order, where, limit, q_rows, k_rows)


SEQ = ("y", "z", "core")
PLANE = ("y", "z")
SIDE = 4


def exchanged(array, axis):
    return lax.all_to_all(array, axis, 0, 0, tiled=True)


def shifted(array, axis, by):
    size = lax.axis_size(axis)
    return lax.ppermute(array, axis, [(i, (i + by) % size) for i in range(size)])


def summed(block, axis):
    size = lax.axis_size(axis)
    me = lax.axis_index(axis)
    total = lax.dynamic_index_in_dim(block, me, 0, keepdims=False)
    for by in range(1, size):
        part = lax.dynamic_index_in_dim(block, lax.rem(me + by, size), 0, keepdims=False)
        total = total + shifted(part, axis, by)
    return total


def in_three(array):
    high = lax.reduce_precision(array, 8, 7)
    middle = lax.reduce_precision(array - high, 8, 7)
    low = array - high - middle
    return jnp.concatenate([high, middle, low], axis=-1).astype(jnp.bfloat16)


def from_three(parts):
    wide = parts.astype(jnp.float32)
    size = wide.shape[-1] // 3
    return wide[..., :size] + wide[..., size : 2 * size] + wide[..., 2 * size :]


def on_device(queries, keys, values, lengths, block_pos, w_in, b_in, output_weight, output_bias):
    q_rows = queries[0]
    k_rows = keys[0]
    v_rows = values[0]
    rows = q_rows.shape[0]
    seq = lax.axis_size(SEQ)
    chips = lax.axis_size(PLANE)
    cores = lax.axis_size("core")
    batch = lax.axis_size("batch")
    heads_kv = output_weight.shape[1]
    hidden = output_weight.shape[0]
    head_size = k_rows.shape[1] // heads_kv
    group = q_rows.shape[1] // k_rows.shape[1]
    heads = heads_kv * group
    total = rows * seq
    order = block_pos[0]
    limit = lengths[0]
    places = jnp.arange(seq, dtype=jnp.int32)
    where = jnp.sum(jnp.where(order[None, :] == places[:, None], places[None, :], 0), axis=1).astype(jnp.int32)
    chip = lax.axis_index(PLANE)
    core = lax.axis_index("core")

    by_head = jnp.moveaxis(q_rows.reshape(rows, heads, head_size), 1, 0)
    keys_by_head = jnp.moveaxis(k_rows.reshape(rows, heads_kv, head_size), 1, 0)
    keys_by_head = jnp.broadcast_to(keys_by_head[:, None], (heads_kv, group, rows, head_size)).reshape(
        heads, rows, head_size
    )
    both = exchanged(jnp.stack([by_head, keys_by_head], axis=1), SEQ)

    features = jnp.concatenate([q_rows, k_rows, v_rows], axis=1)
    pre = jnp.dot(features, w_in, preferred_element_type=jnp.float32) + b_in
    sig = jax.nn.sigmoid(pre)
    act = (pre * sig).astype(jnp.bfloat16)
    pred = jnp.dot(act, output_weight, preferred_element_type=jnp.float32) + output_bias
    slope = sig * (1.0 + pre * (1.0 - sig))
    largest = jnp.maximum(jnp.max(jnp.abs(slope), axis=1, keepdims=True), 1e-30)
    slope = (slope / largest).astype(jnp.float16)

    width = features.shape[1] // chips
    part = hidden // chips
    carried = jnp.concatenate(
        [
            features.reshape(rows, chips, width),
            act.reshape(rows, chips, part),
            jnp.broadcast_to(
                jnp.pad(
                    jnp.concatenate([in_three(pred), in_three(largest)], axis=1), ((0, 0), (0, part - 3 * heads_kv - 3))
                )[:, None],
                (rows, chips, part),
            ),
        ],
        axis=2,
    )
    own_q = both[:, 0].reshape(total, head_size)
    own_k = both[:, 1].reshape(total, head_size)
    own_q, own_k, slope, carried = lax.optimization_barrier((own_q, own_k, slope, jnp.moveaxis(carried, 1, 0)))
    spread = exchanged(carried, PLANE)
    partial = head_mass(order, where, lengths, own_q, own_k, 1.0 / math.sqrt(head_size))

    to_cores = jnp.moveaxis(partial.reshape(chips, cores, rows), 1, 0)
    to_all = jnp.broadcast_to(to_cores[None], (chips, cores, chips, rows)).reshape(seq, chips, rows)
    slope, to_all = lax.optimization_barrier((slope, to_all))
    arrived = exchanged(to_all, SEQ)
    slopes = lax.all_gather(slope, PLANE, axis=0, tiled=True)
    slopes, arrived = lax.optimization_barrier((slopes, arrived))
    mass = jnp.sum(arrived.reshape(heads_kv, group, chips * rows), axis=1)
    labels = jnp.log1p(mass).T

    spread = spread.reshape(chips * rows, width + 2 * part)
    feats = spread[:, :width]
    acts = spread[:, width : width + part]
    predicted = from_three(spread[:, width + part : width + part + 3 * heads_kv])
    factor = from_three(spread[:, width + part + 3 * heads_kv : width + part + 3 * heads_kv + 3])
    offsets = jnp.arange(rows, dtype=jnp.int32)
    blocks = lax.dynamic_index_in_dim(order.reshape(chips, cores), core, 1, keepdims=False)
    position = (blocks[:, None] * rows + offsets[None, :]).reshape(-1)
    live = (position < limit).astype(jnp.float32)
    norm = 1.0 / math.sqrt(batch * total)
    resid = ((predicted - labels) * live[:, None] * norm).astype(jnp.bfloat16)
    back = lax.dot_general(
        resid, output_weight, (((1,), (1,)), ((), ())), preferred_element_type=jnp.float32
    )
    delta = (back * (slopes.astype(jnp.float32) * factor)).astype(jnp.bfloat16)
    block = lax.dot_general(
        feats, delta, (((0,), (0,)), ((), ())), preferred_element_type=jnp.float32
    )
    block = summed(block.reshape(cores, width // cores, hidden), "core")

    out_part = lax.dot_general(acts, resid, (((0,), (0,)), ((), ())), preferred_element_type=jnp.float32)
    b_part = lax.dynamic_index_in_dim(
        jnp.sum(delta.astype(jnp.float32), axis=0).reshape(chips, part), chip, 0, keepdims=False
    )
    small = jnp.concatenate([out_part.ravel(), b_part, jnp.sum(resid.astype(jnp.float32), axis=0)])
    size = small.shape[0]
    small = jnp.pad(small, (0, -size % 128))
    small = exchanged(jnp.broadcast_to(small[None], (seq, small.shape[0])), SEQ)
    small = jnp.sum(small.reshape(chips, cores, small.shape[1]), axis=1)
    across = small.shape[1]
    small = jnp.pad(small.ravel(), (0, -small.size % hidden)).reshape(-1, hidden)
    block = block.reshape(batch, width // (cores * batch), hidden)
    ending = jnp.concatenate([block, jnp.broadcast_to(small[None], (batch, *small.shape))], axis=1)
    ending = summed(ending, "batch")
    grad_w_in = ending[: block.shape[1]]
    small = ending[block.shape[1] :].ravel()[: chips * across].reshape(chips, across)
    output_weight_gradient = small[:, : part * heads_kv].reshape(hidden, heads_kv)
    grad_b_in = small[:, part * heads_kv : part * heads_kv + part].reshape(hidden)
    output_bias_gradient = small[0, part * heads_kv + part : size]
    return (grad_w_in, grad_b_in, output_weight_gradient, output_bias_gradient)


def solution(mesh):
    cores = mesh.shape["seq"] // (SIDE * SIDE)
    fine = Mesh(
        mesh.devices.reshape(SIDE, SIDE, cores, mesh.shape["batch"]), SEQ + ("batch",)
    )
    return jax.shard_map(
        on_device,
        mesh=fine,
        in_specs=(
            P("batch", SEQ, None),
            P("batch", SEQ, None),
            P("batch", SEQ, None),
            P("batch"),
            P("batch", None),
            P(),
            P(),
            P(),
            P(),
        ),
        out_specs=(P(SEQ + ("batch",), None), P(), P(), P()),
        check_vma=False,
    )
```

time: 204 us -> 193 us (0.946)
  blocking collectives: 0 us -> 68.5 us
  waiting for transfers between devices: 74.5 us -> 30.4 us
  starting transfers between devices: 64.9 us -> 22.3 us
  between operations: 14.9 us -> 1.7 us
  Pallas kernels: 16.3 us -> 24.3 us
  local copies, waits for them, and re-layouts: 13.9 us -> 21.8 us
  other arithmetic: 4.92 us -> 9.15 us
    all_gather x0 -> x1, blocking collectives: none -> 56.6 us  [on_device(): slopes = lax.all_gather(slope, PLANE, axis=0, tiled=True)]
    all_to_all x6 -> x3, starting transfers between devices: 64.9 us -> 17.8 us  [exchanged(): return lax.all_to_all(array, axis, 0, 0, tiled=True)]
    all_to_all x6 -> x3, waiting for transfers between devices: 62.7 us -> 19.3 us  [exchanged(): return lax.all_to_all(array, axis, 0, 0, tiled=True)]
    all_to_all x0 -> x1, blocking collectives: none -> 11.9 us  [exchanged(): return lax.all_to_all(array, axis, 0, 0, tiled=True)]
    all_gather x1 -> x0, waiting for transfers between devices: 11.7 us -> none  [on_device(): every_delta = lax.all_gather(delta, 'seq', axis=0, tiled=True)]
    ppermute x0 -> x4, waiting for transfers between devices: none -> 11.1 us  [shifted(): lax.ppermute(array, axis, [(i, (i + by) % size) for i in range(size)])]
    pallas_call x1, Pallas kernels: 16.3 us -> 24.3 us  [head_mass(): pl.pallas_call(functools.partial(mass_kernel, scale=scale), out_shape=jax...]
    dot_general x2, matrix products: 6.8 us -> 2.11 us  [the longest x1 1.81 us: on_device(): lax.dot_general(feats, delta, (((0,), (0,)), ((), ())), preferred_element...]
  transfers between devices with their start and end apart: 7 -> 7, of which waited for: 5 -> 5; matrix products, arithmetic and copies ran while one was open for 12% -> 10% of each run, Pallas kernels for 0% -> 0%
where the time goes in v2:
time: 193 us; the launch traced here: 192 us
  blocking collectives  68.5 us (35%)
  waiting for transfers between devices  30.4 us (16%)
  Pallas kernels  24.3 us (13%)
  starting transfers between devices  22.3 us (12%)
  local copies, waits for them, and re-layouts  21.8 us (11%)
  matrix products  13.6 us (7%)
  other arithmetic  9.15 us (5%)
    all_gather x1, blocking collectives, on_device(): slopes = lax.all_gather(slope, PLANE, axis=0, tiled=True)  56.6 us
    pallas_call x1, Pallas kernels, head_mass(): pl.pallas_call(functools.partial(mass_kernel, scale=scale), out_shape=jax...  24.3 us
    all_to_all x3, waiting for transfers between devices, exchanged(): return lax.all_to_all(array, axis, 0, 0, tiled=True)  19.3 us
    all_to_all x3, starting transfers between devices, exchanged(): return lax.all_to_all(array, axis, 0, 0, tiled=True)  17.8 us
    all_to_all x1, blocking collectives, exchanged(): return lax.all_to_all(array, axis, 0, 0, tiled=True)  11.9 us
    ppermute x4, waiting for transfers between devices, shifted(): lax.ppermute(array, axis, [(i, (i + by) % size) for i in range(size)])  11.1 us
    unnamed x23, local copies, waits for them, and re-layouts  8.22 us
    dot_general x1, matrix products, on_device(): pre = jnp.dot(features, w_in, preferred_element_type=jnp.float32) + b_in  6.75 us
  transfers between devices with their start and end apart: 7, of which 5 were waited for; matrix products, arithmetic and copies ran while one was open for 10% of the time, Pallas kernels for 0%

profile of v2, /device:TPU:0, one launch (start us, length us, event | category | flops | bytes accessed | tf_op | source)
XLA Modules:
  0.0 191.6 jit_solution(7389772183139515424)
XLA Ops:
  1.9 1.6 copy.81
  4.0 2.8 %copy.83 = bf16[32,2,128,128]{3,2,1,0:T(8,128)(2,1)} copy(bf16[32,2,128,128]{2,3,0,1:T(8,128)(2,1)S(1)} %pad_maximum_fusion) | data formatting | bytes 4194304 | tf_op jit(solution)/shard_map/stack | solution.py:191
  6.8 8.6 %all-to-all-start = ((bf16[32,2,128,128]{3,2,1,0:T(8,128)(2,1)}), bf16[32,2,128,128]{3,2,1,0:T(8,128)(2,1)S(1)}, u32[]{:S(2)}, u32[]{:S(2)}) async-start(bf16[32,2,128,128]{3,2,1,0:T(8,128)(2,1)} %copy.83), calls=%async_computation | async-start | bytes 4194304 | tf_op jit(solution)/shard_map/all_to_all | solution.py:133
  16.5 1.8 copy.86
  18.3 6.8 %abs_reduce_fusion = (f32[128]{0:T(128)S(1)}, f32[128,1024]{1,0:T(8,128)S(1)}) fusion(f32[1024]{0:T(1024)S(1)} %copy-done.6, bf16[6144,1024]{1,0:T(8,128)(2,1)} %param.14, bf16[128,1024]{0,1:T(8,128)(2,1)} %bitcast.91, bf16[128,1024]{0,1:T(8,128)(2,1)S(1)} %bitcast.89, bf16[128,4096]{0,1:T(8,128)(2,1)S(1)} %bitcast.77), kind=kOutput, calls=%fused_computation.27 | convolution fusion | flops 1616641920 | bytes 14684672 | tf_op jit(solution)/shard_map/dot_general | solution.py:194
  26.1 1.8 copy.87
  31.0 1.5 maximum_bitcast_fusion
  32.5 11.7 %all-to-all-done = bf16[32,2,128,128]{3,2,1,0:T(8,128)(2,1)S(1)} async-done(((bf16[32,2,128,128]{3,2,1,0:T(8,128)(2,1)}), bf16[32,2,128,128]{3,2,1,0:T(8,128)(2,1)S(1)}, u32[]{:S(2)}, u32[]{:S(2)}) %all-to-all-start) | async-done | bytes 2097184 | tf_op jit(solution)/shard_map/all_to_all | solution.py:133
  44.5 24.3 %head_mass.1 = f32[32,128]{1,0:T(8,128)S(1)} custom-call(s32[32]{0:T(128)S(1)} %bitcast.75, s32[32]{0:T(128)S(1)} %select_reduce_fusion.where_ref, s32[1]{0:T(128)} %copy.101.limit_ref, bf16[4096,128]{1,0:T(8,128)(2,1)S(1)} %bitcast.72, bf16[4096,128]{1,0:T(8,128)(2,1)S(1)} %bitcast.71), custom_call_target="tpu_custom_call" | custom-call | flops 4294967296 | bytes 2097152 | tf_op jit(solution)/shard_map/head_mass/pallas_call | solution.py:109
  68.8 11.9 %all_to_all.21 = f32[32,16,128]{2,1,0:T(8,128)S(1)} all-to-all(f32[32,16,128]{2,1,0:T(8,128)S(1)} %bitcast.95), channel_id=1, replica_groups=mesh['y'=4,'z'=4,'core'=2,'batch'=4] {'y','z','core'}, dimensions={0} | all-to-all | bytes 524288 | tf_op jit(solution)/shard_map/all_to_all | solution.py:133
  80.7 3.8 %all-to-all-start.1 = ((bf16[16,128,512]{1,2,0:T(8,128)(2,1)}), bf16[16,128,512]{1,2,0:T(8,128)(2,1)S(1)}, u32[]{:S(2)}, u32[]{:S(2)}) async-start(bf16[16,128,512]{1,2,0:T(8,128)(2,1)} %maximum_bitcast_fusion), calls=%async_computation.1 | async-start | bytes 4194304 | tf_op jit(solution)/shard_map/all_to_all | solution.py:133
  86.1 56.6 %all-gather.1 = f16[2048,1024]{1,0:T(8,128)(2,1)} all-gather(f16[128,1024]{1,0:T(8,128)(2,1)S(1)} %copy-done.5), channel_id=1, replica_groups=mesh['y'=4,'z'=4,'core'=2,'batch'=4] {'y','z'}, dimensions={0}, use_global_device_ids=true | all-gather | bytes 4456448 | tf_op jit(solution)/shard_map/all_gather | solution.py:227
  143.0 2.6 %copy.88 = bf16[16,128,512]{2,1,0:T(8,128)(2,1)} copy(bf16[16,128,512]{1,2,0:T(8,128)(2,1)S(1)} %all-to-all-done.1) | data formatting | bytes 4194304 | tf_op jit(solution)/shard_map/all_to_all | solution.py:133
  145.6 1.2 slice_convert_fusion
  146.8 1.2 slice.71
  149.5 3.6 %convert_reduce_fusion = (f32[1024]{0:T(1024)S(1)}, bf16[2048,1024]{1,0:T(8,128)(2,1)S(1)}) fusion(f32[2048]{0:T(1024)S(1)} %fusion.2, f16[2048,1024]{1,0:T(8,128)(2,1)} %all-gather.1, bf16[2048,8]{0,1:T(8,128)(2,1)S(1)} %get-tuple-element.49, bf16[1024,8]{0,1:T(8,128)(2,1)S(1)} %copy-done), kind=kOutput, calls=%fused_computation | convolution fusion | flops 46136320 | bytes 8450048 | tf_op jit(solution)/shard_map/dot_general | solution.py:243
  153.1 1.8 fusion
  158.2 5.3 %all-to-all-start.3 = ((f32[32,1,640]{2,1,0:T(1,128)}), f32[32,1,640]{2,1,0:T(1,128)S(1)}, u32[]{:S(2)}, u32[]{:S(2)}) async-start(f32[32,1,640]{2,1,0:T(1,128)} %broadcast_in_dim.29), calls=%async_computation.3 | async-start | bytes 163840 | tf_op jit(solution)/shard_map/all_to_all | solution.py:133
  163.6 7.5 %all-to-all-done.3 = f32[32,1,640]{2,1,0:T(1,128)S(1)} async-done(((f32[32,1,640]{2,1,0:T(1,128)}), f32[32,1,640]{2,1,0:T(1,128)S(1)}, u32[]{:S(2)}, u32[]{:S(2)}) %all-to-all-start.3) | async-done | bytes 81952 | tf_op jit(solution)/shard_map/all_to_all | solution.py:133
  173.0 3.1 %collective-permute-start.2 = (f32[58,1024]{1,0:T(8,128)S(1)}, f32[58,1024]{1,0:T(8,128)S(1)}, u32[]{:S(2)}, u32[]{:S(2)}) collective-permute-start(f32[58,1024]{1,0:T(8,128)S(1)} %get-tuple-element.53), channel_id=1, source_target_pairs={{0,2},{1,3},{2,0},{3,1},{4,6},{5,7},{6,4},{7,5},{8,10},{9,11},{10,... | collective-permute-start | bytes 712712 | tf_op jit(solution)/shard_map/ppermute | solution.py:138
  176.1 1.3 collective-permute-start.1
  177.4 4.7 %collective-permute-done.3 = f32[58,1024]{1,0:T(8,128)S(1)} collective-permute-done((f32[58,1024]{1,0:T(8,128)S(1)}, f32[58,1024]{1,0:T(8,128)S(1)}, u32[]{:S(2)}, u32[]{:S(2)}) %collective-permute-start.3) | collective-permute-done | bytes 237600 | tf_op jit(solution)/shard_map/ppermute | solution.py:138
  182.1 1.6 collective-permute-done.2
  183.8 4.7 %collective-permute-done.1 = f32[58,1024]{1,0:T(8,128)S(1)} collective-permute-done((f32[58,1024]{1,0:T(8,128)S(1)}, f32[58,1024]{1,0:T(8,128)S(1)}, u32[]{:S(2)}, u32[]{:S(2)}) %collective-permute-start.1) | collective-permute-done | bytes 237600 | tf_op jit(solution)/shard_map/ppermute | solution.py:138
  (72 shorter events, 17.8 us)
Async XLA Ops:
  0.6 27.9 %copy-start = (bf16[1024,8]{0,1:T(8,128)(2,1)S(1)}, bf16[1024,8]{0,1:T(8,128)(2,1)}, u32[]{:S(2)}) copy-start(bf16[1024,8]{0,1:T(8,128)(2,1)} %param.16) | copy-start | bytes 49156
  6.7 11.5 %copy-start.6 = (f32[1024]{0:T(1024)S(1)}, f32[1024]{0:T(1024)}, u32[]{:S(2)}) copy-start(f32[1024]{0:T(1024)} %param.15) | copy-start | bytes 12292
  6.8 37.5 %all-to-all-start = ((bf16[32,2,128,128]{3,2,1,0:T(8,128)(2,1)}), bf16[32,2,128,128]{3,2,1,0:T(8,128)(2,1)S(1)}, u32[]{:S(2)}, u32[]{:S(2)}) async-start(bf16[32,2,128,128]{3,2,1,0:T(8,128)(2,1)} %copy.83), calls=%async_computation | async-start | bytes 4194304 | tf_op jit(solution)/shard_map/all_to_all | solution.py:133
  18.3 10.3 %copy-start.7 = (f32[8]{0:T(128)S(1)}, f32[8]{0:T(128)}, u32[]{:S(2)}) copy-start(f32[8]{0:T(128)} %param.17) | copy-start | bytes 100
  18.3 11.5 %copy-start.1 = (s32[1,32]{1,0:T(1,128)S(1)}, s32[1,32]{1,0:T(1,128)}, u32[]{:S(2)}) copy-start(s32[1,32]{1,0:T(1,128)} %param.13) | copy-start | bytes 388
  29.8 1.3 copy-start.4
  80.7 5.4 %copy-start.5 = (f16[128,1024]{1,0:T(8,128)(2,1)S(1)}, f16[128,1024]{1,0:T(8,128)(2,1)}, u32[]{:S(2)}) copy-start(f16[128,1024]{1,0:T(8,128)(2,1)} %get-tuple-element.16) | copy-start | bytes 786436
  80.7 62.3 %all-to-all-start.1 = ((bf16[16,128,512]{1,2,0:T(8,128)(2,1)}), bf16[16,128,512]{1,2,0:T(8,128)(2,1)S(1)}, u32[]{:S(2)}, u32[]{:S(2)}) async-start(bf16[16,128,512]{1,2,0:T(8,128)(2,1)} %maximum_bitcast_fusion), calls=%async_computation.1 | async-start | bytes 4194304 | tf_op jit(solution)/shard_map/all_to_all | solution.py:133
  149.5 3.6 %copy-start.2 = (bf16[16,128,512]{2,1,0:T(8,128)(2,1)S(1)}, bf16[16,128,512]{2,1,0:T(8,128)(2,1)}, u32[]{:S(2)}) copy-start(bf16[16,128,512]{2,1,0:T(8,128)(2,1)} %copy.88) | copy-start | bytes 6291460
  154.9 1.2 copy-start.3
  157.0 14.5 %collective-permute-start = (f32[192,1024]{1,0:T(8,128)}, f32[192,1024]{1,0:T(8,128)S(1)}, u32[]{:S(2)}, u32[]{:S(2)}) collective-permute-start(f32[192,1024]{1,0:T(8,128)} %dynamic-slice_bitcast_fusion), channel_id=1, source_target_pairs={{0,4},{4,0},{1,5},{5,1},{2,6},{6,2},{3,7},{7,3},{8,12},{12,8},{9,1... | collective-permute-start | bytes 2359304 | tf_op jit(solution)/shard_map/ppermute | solution.py:138
  158.2 12.9 %all-to-all-start.3 = ((f32[32,1,640]{2,1,0:T(1,128)}), f32[32,1,640]{2,1,0:T(1,128)S(1)}, u32[]{:S(2)}, u32[]{:S(2)}) async-start(f32[32,1,640]{2,1,0:T(1,128)} %broadcast_in_dim.29), calls=%async_computation.3 | async-start | bytes 163840 | tf_op jit(solution)/shard_map/all_to_all | solution.py:133
  172.9 9.2 %collective-permute-start.3 = (f32[58,1024]{1,0:T(8,128)S(1)}, f32[58,1024]{1,0:T(8,128)S(1)}, u32[]{:S(2)}, u32[]{:S(2)}) collective-permute-start(f32[58,1024]{1,0:T(8,128)S(1)} %get-tuple-element.54), channel_id=1, source_target_pairs={{0,3},{1,0},{2,1},{3,2},{4,7},{5,4},{6,5},{7,6},{8,11},{9,8},{10,9... | collective-permute-start | bytes 712712 | tf_op jit(solution)/shard_map/ppermute | solution.py:138
  173.0 10.8 %collective-permute-start.2 = (f32[58,1024]{1,0:T(8,128)S(1)}, f32[58,1024]{1,0:T(8,128)S(1)}, u32[]{:S(2)}, u32[]{:S(2)}) collective-permute-start(f32[58,1024]{1,0:T(8,128)S(1)} %get-tuple-element.53), channel_id=1, source_target_pairs={{0,2},{1,3},{2,0},{3,1},{4,6},{5,7},{6,4},{7,5},{8,10},{9,11},{10,... | collective-permute-start | bytes 712712 | tf_op jit(solution)/shard_map/ppermute | solution.py:138
  176.1 12.4 %collective-permute-start.1 = (f32[58,1024]{1,0:T(8,128)S(1)}, f32[58,1024]{1,0:T(8,128)S(1)}, u32[]{:S(2)}, u32[]{:S(2)}) collective-permute-start(f32[58,1024]{1,0:T(8,128)S(1)} %get-tuple-element.52), channel_id=1, source_target_pairs={{0,1},{1,2},{2,3},{3,0},{4,5},{5,6},{6,7},{7,4},{8,9},{9,10},{10,1... | collective-permute-start | bytes 712712 | tf_op jit(solution)/shard_map/ppermute | solution.py:138

commit v3 on v2

--- a/solution.py
+++ b/solution.py
@@ -14,16 +14,17 @@
 KEYS = 512
 
 
-def mass_kernel(order_ref, where_ref, limit_ref, q_ref, k_ref, out_ref, keys, scores, col, *, scale):
-    blocks = q_ref.shape[0] // BLOCK
+def mass_kernel(order_ref, limit_ref, both_ref, out_ref, where_ref, keys, scores, col, *, scale):
+    blocks = both_ref.shape[0]
     limit = limit_ref[0]
     factor = scale * math.log2(math.e)
     diagonal = QUERIES // KEYS
     lanes = QUERIES // BLOCK
 
-    def by_position(p, carry):
-        start = pl.multiple_of(where_ref[p] * BLOCK, BLOCK)
-        keys[pl.ds(pl.multiple_of(p * BLOCK, BLOCK), BLOCK), :] = k_ref[pl.ds(start, BLOCK), :]
+    def by_position(i, carry):
+        p = order_ref[i]
+        where_ref[p] = i
+        keys[pl.ds(pl.multiple_of(p * BLOCK, BLOCK), BLOCK), :] = both_ref[i, 1]
         return carry
 
     lax.fori_loop(0, blocks, by_position, 0)
@@ -42,9 +43,7 @@
         col[c] += part
 
     def query_block(r, weight):
-        parts = [
-            q_ref[pl.ds(pl.multiple_of(where_ref[r * lanes + i] * BLOCK, BLOCK), BLOCK), :] for i in range(lanes)
-        ]
+        parts = [both_ref[where_ref[r * lanes + i], 0] for i in range(lanes)]
         q_rows = jnp.concatenate(parts, axis=0)
         slot = lax.rem(r, 2)
 
@@ -102,16 +101,18 @@
     lax.fori_loop(0, blocks, store, 0)
 
 
-def head_mass(order, where, limit, q_rows, k_rows, scale):
-    tokens, size = q_rows.shape
+def head_mass(order, limit, both, scale):
+    blocks, _, rows, size = both.shape
+    tokens = blocks * rows
     smem = pl.BlockSpec(memory_space=pltpu.SMEM)
     vmem = pl.BlockSpec(memory_space=pltpu.VMEM)
     return pl.pallas_call(
         functools.partial(mass_kernel, scale=scale),
-        out_shape=jax.ShapeDtypeStruct((tokens // BLOCK, BLOCK), jnp.float32),
-        in_specs=[smem, smem, smem, vmem, vmem],
+        out_shape=jax.ShapeDtypeStruct((blocks, BLOCK), jnp.float32),
+        in_specs=[smem, smem, vmem],
         out_specs=vmem,
         scratch_shapes=[
+            pltpu.SMEM((blocks,), jnp.int32),
             pltpu.VMEM((tokens, size), jnp.bfloat16),
             pltpu.VMEM((2, tokens // KEYS, KEYS, QUERIES), jnp.float32),
             pltpu.VMEM((tokens // KEYS, KEYS, BLOCK), jnp.float32),
@@ -121,7 +122,29 @@
             flops=2 * tokens * tokens * size, bytes_accessed=4 * tokens * size, transcendentals=tokens * tokens // 2
         ),
         name="head_mass",
-    )(order, where, limit, q_rows, k_rows)
+    )(order, limit, both)
+
+
+def by_head_kernel(q_ref, k_ref, out_ref):
+    heads, _, _, size = out_ref.shape
+    group = q_ref.shape[1] // k_ref.shape[1]
+    for h in range(heads):
+        g = h // group
+        out_ref[h, 0] = q_ref[:, h * size : (h + 1) * size]
+        out_ref[h, 1] = k_ref[:, g * size : (g + 1) * size]
+
+
+def by_head(q_rows, k_rows, size):
+    rows, width = q_rows.shape
+    vmem = pl.BlockSpec(memory_space=pltpu.VMEM)
+    return pl.pallas_call(
+        by_head_kernel,
+        out_shape=jax.ShapeDtypeStruct((width // size, 2, rows, size), q_rows.dtype),
+        in_specs=[vmem, vmem],
+        out_specs=vmem,
+        compiler_params=pltpu.CompilerParams(vmem_limit_bytes=16 * 1024 * 1024),
+        name="by_head",
+    )(q_rows, k_rows)
 
 
 SEQ = ("y", "z", "core")
@@ -174,21 +197,13 @@
     hidden = output_weight.shape[0]
     head_size = k_rows.shape[1] // heads_kv
     group = q_rows.shape[1] // k_rows.shape[1]
-    heads = heads_kv * group
     total = rows * seq
     order = block_pos[0]
     limit = lengths[0]
-    places = jnp.arange(seq, dtype=jnp.int32)
-    where = jnp.sum(jnp.where(order[None, :] == places[:, None], places[None, :], 0), axis=1).astype(jnp.int32)
     chip = lax.axis_index(PLANE)
     core = lax.axis_index("core")
 
-    by_head = jnp.moveaxis(q_rows.reshape(rows, heads, head_size), 1, 0)
-    keys_by_head = jnp.moveaxis(k_rows.reshape(rows, heads_kv, head_size), 1, 0)
-    keys_by_head = jnp.broadcast_to(keys_by_head[:, None], (heads_kv, group, rows, head_size)).reshape(
-        heads, rows, head_size
-    )
-    both = exchanged(jnp.stack([by_head, keys_by_head], axis=1), SEQ)
+    both = exchanged(by_head(q_rows, k_rows, head_size), SEQ)
 
     features = jnp.concatenate([q_rows, k_rows, v_rows], axis=1)
     pre = jnp.dot(features, w_in, preferred_element_type=jnp.float32) + b_in
@@ -214,11 +229,9 @@
         ],
         axis=2,
     )
-    own_q = both[:, 0].reshape(total, head_size)
-    own_k = both[:, 1].reshape(total, head_size)
-    own_q, own_k, slope, carried = lax.optimization_barrier((own_q, own_k, slope, jnp.moveaxis(carried, 1, 0)))
+    both, slope, carried = lax.optimization_barrier((both, slope, jnp.moveaxis(carried, 1, 0)))
     spread = exchanged(carried, PLANE)
-    partial = head_mass(order, where, lengths, own_q, own_k, 1.0 / math.sqrt(head_size))
+    partial = head_mass(order, lengths, both, 1.0 / math.sqrt(head_size))
 
     to_cores = jnp.moveaxis(partial.reshape(chips, cores, rows), 1, 0)
     to_all = jnp.broadcast_to(to_cores[None], (chips, cores, chips, rows)).reshape(seq, chips, rows)
@@ -244,11 +257,6 @@
         resid, output_weight, (((1,), (1,)), ((), ())), preferred_element_type=jnp.float32
     )
     delta = (back * (slopes.astype(jnp.float32) * factor)).astype(jnp.bfloat16)
-    block = lax.dot_general(
-        feats, delta, (((0,), (0,)), ((), ())), preferred_element_type=jnp.float32
-    )
-    block = summed(block.reshape(cores, width // cores, hidden), "core")
-
     out_part = lax.dot_general(acts, resid, (((0,), (0,)), ((), ())), preferred_element_type=jnp.float32)
     b_part = lax.dynamic_index_in_dim(
         jnp.sum(delta.astype(jnp.float32), axis=0).reshape(chips, part), chip, 0, keepdims=False
@@ -257,14 +265,13 @@
     size = small.shape[0]
     small = jnp.pad(small, (0, -size % 128))
     small = exchanged(jnp.broadcast_to(small[None], (seq, small.shape[0])), SEQ)
+    block = lax.dot_general(
+        feats, delta, (((0,), (0,)), ((), ())), preferred_element_type=jnp.float32
+    )
+    block = summed(block.reshape(cores, width // cores, hidden), "core")
+    grad_w_in = summed(block.reshape(batch, width // (cores * batch), hidden), "batch")
     small = jnp.sum(small.reshape(chips, cores, small.shape[1]), axis=1)
-    across = small.shape[1]
-    small = jnp.pad(small.ravel(), (0, -small.size % hidden)).reshape(-1, hidden)
-    block = block.reshape(batch, width // (cores * batch), hidden)
-    ending = jnp.concatenate([block, jnp.broadcast_to(small[None], (batch, *small.shape))], axis=1)
-    ending = summed(ending, "batch")
-    grad_w_in = ending[: block.shape[1]]
-    small = ending[block.shape[1] :].ravel()[: chips * across].reshape(chips, across)
+    small = small + sum(shifted(small, "batch", by) for by in range(1, batch))
     output_weight_gradient = small[:, : part * heads_kv].reshape(hidden, heads_kv)
     grad_b_in = small[:, part * heads_kv : part * heads_kv + part].reshape(hidden)
     output_bias_gradient = small[0, part * heads_kv + part : size]

time: 193 us -> 188 us (0.974)
  blocking collectives: 68.5 us -> 81.2 us
  local copies, waits for them, and re-layouts: 21.8 us -> 12.4 us
  waiting for transfers between devices: 30.4 us -> 22 us
    all_to_all x1 -> x2, blocking collectives: 11.9 us -> 24.6 us  [exchanged(): return lax.all_to_all(array, axis, 0, 0, tiled=True)]
    all_to_all x3 -> x2, waiting for transfers between devices: 19.3 us -> 12.1 us  [exchanged(): return lax.all_to_all(array, axis, 0, 0, tiled=True)]
    all_to_all x3 -> x2, starting transfers between devices: 17.8 us -> 12.2 us  [exchanged(): return lax.all_to_all(array, axis, 0, 0, tiled=True)]
    ppermute x4 -> x7, starting transfers between devices: 4.5 us -> 9.82 us  [shifted(): lax.ppermute(array, axis, [(i, (i + by) % size) for i in range(size)])]
    unnamed x23 -> x26, local copies, waits for them, and re-layouts: 8.22 us -> 5 us
    another operation x2 -> x0, local copies, waits for them, and re-layouts: 2.77 us -> none  [the longest x1 2.76 us: on_device(): both = exchanged(jnp.stack([by_head, keys_by_head], axis=1), SEQ)]
    all_to_all x1 -> x0, local copies, waits for them, and re-layouts: 2.62 us -> none  [exchanged(): return lax.all_to_all(array, axis, 0, 0, tiled=True)]
    reshape x0 -> x2, local copies, waits for them, and re-layouts: none -> 2.19 us  [the longest x1 1.96 us: on_device(): act.reshape(rows, chips, part)]
  transfers between devices with their start and end apart: 7 -> 9, of which waited for: 5 -> 6; matrix products, arithmetic and copies ran while one was open for 10% -> 11% of each run, Pallas kernels for 0% -> 0%
where the time goes in v3:
time: 188 us; the launch traced here: 187 us
  blocking collectives  81.2 us (43%)
  Pallas kernels  25.8 us (14%)
  starting transfers between devices  22 us (12%)
  waiting for transfers between devices  22 us (12%)
  matrix products  13.3 us (7%)
  local copies, waits for them, and re-layouts  12.4 us (7%)
  other arithmetic  8.71 us (5%)
    all_gather x1, blocking collectives, on_device(): slopes = lax.all_gather(slope, PLANE, axis=0, tiled=True)  56.6 us
    all_to_all x2, blocking collectives, exchanged(): return lax.all_to_all(array, axis, 0, 0, tiled=True)  24.6 us
    pallas_call x1, Pallas kernels, head_mass(): pl.pallas_call(functools.partial(mass_kernel, scale=scale), out_shape=jax...  24.2 us
    all_to_all x2, starting transfers between devices, exchanged(): return lax.all_to_all(array, axis, 0, 0, tiled=True)  12.2 us
    all_to_all x2, waiting for transfers between devices, exchanged(): return lax.all_to_all(array, axis, 0, 0, tiled=True)  12.1 us
    ppermute x7, waiting for transfers between devices, shifted(): lax.ppermute(array, axis, [(i, (i + by) % size) for i in range(size)])  9.95 us
    ppermute x7, starting transfers between devices, shifted(): lax.ppermute(array, axis, [(i, (i + by) % size) for i in range(size)])  9.82 us
    dot_general x1, matrix products, on_device(): pre = jnp.dot(features, w_in, preferred_element_type=jnp.float32) + b_in  6.7 us
  transfers between devices with their start and end apart: 9, of which 6 were waited for; matrix products, arithmetic and copies ran while one was open for 11% of the time, Pallas kernels for 0%

profile of v3, /device:TPU:0, one launch (start us, length us, event | category | flops | bytes accessed | tf_op | source)
XLA Modules:
  0.0 187.1 jit_solution(8603601007941902333)
XLA Ops:
  2.8 1.6 by_head.1
  4.5 8.4 %all-to-all-start = ((bf16[32,2,128,128]{3,2,1,0:T(8,128)(2,1)}), bf16[32,2,128,128]{3,2,1,0:T(8,128)(2,1)S(1)}, u32[]{:S(2)}, u32[]{:S(2)}) async-start(bf16[32,2,128,128]{3,2,1,0:T(8,128)(2,1)} %by_head.1), calls=%async_computation | async-start | bytes 4194304 | tf_op jit(solution)/shard_map/all_to_all | solution.py:156
  13.0 6.7 %abs_reduce_fusion = (f32[128]{0:T(128)S(1)}, f32[128,1024]{1,0:T(8,128)S(1)}) fusion(f32[1024]{0:T(1024)S(1)} %copy-done.9, bf16[6144,1024]{1,0:T(8,128)(2,1)} %param.14, bf16[128,1024]{1,0:T(8,128)(2,1)} %bitcast.79, bf16[128,1024]{1,0:T(8,128)(2,1)S(1)} %bitcast.63, bf16[128,4096]{1,0:T(8,128)(2,1)S(1)} %bitcast.60), kind=kOutput, calls=%fused_computation.19 | convolution fusion | flops 1616641920 | bytes 14684672 | tf_op jit(solution)/shard_map/dot_general | solution.py:209
  20.7 1.8 copy.40
  23.9 2.0 %copy.43 = bf16[128,16,64]{2,0,1:T(8,128)(2,1)} copy(bf16[128,16,64]{0,2,1:T(8,128)(2,1)} %bitcast.77) | data formatting | bytes 524288 | tf_op jit(solution)/shard_map/reshape | solution.py:222
  28.0 1.7 maximum_bitcast_fusion
  29.8 12.1 %all-to-all-done.both_ref = bf16[32,2,128,128]{3,2,1,0:T(8,128)(2,1)S(1)} async-done(((bf16[32,2,128,128]{3,2,1,0:T(8,128)(2,1)}), bf16[32,2,128,128]{3,2,1,0:T(8,128)(2,1)S(1)}, u32[]{:S(2)}, u32[]{:S(2)}) %all-to-all-start) | async-done | bytes 2097184 | tf_op jit(solution)/shard_map/all_to_all | solution.py:156
  41.8 24.2 %head_mass.1 = f32[32,128]{1,0:T(8,128)S(1)} custom-call(s32[32]{0:T(128)S(1)} %bitcast.66, s32[1]{0:T(128)} %copy.59.limit_ref, bf16[32,2,128,128]{3,2,1,0:T(8,128)(2,1)S(1)} %all-to-all-done.both_ref), custom_call_target="tpu_custom_call" | custom-call | flops 4294967296 | bytes 2097152 | tf_op jit(solution)/shard_map/head_mass/pallas_call | solution.py:109
  66.1 12.1 %all_to_all.21 = f32[32,16,128]{2,1,0:T(8,128)S(1)} all-to-all(f32[32,16,128]{2,1,0:T(8,128)S(1)} %bitcast.78), channel_id=1, replica_groups=mesh['y'=4,'z'=4,'core'=2,'batch'=4] {'y','z','core'}, dimensions={0} | all-to-all | bytes 524288 | tf_op jit(solution)/shard_map/all_to_all | solution.py:156
  78.2 3.7 %all-to-all-start.1 = ((bf16[16,128,512]{2,1,0:T(8,128)(2,1)}), bf16[16,128,512]{2,1,0:T(8,128)(2,1)S(1)}, u32[]{:S(2)}, u32[]{:S(2)}) async-start(bf16[16,128,512]{2,1,0:T(8,128)(2,1)} %maximum_bitcast_fusion), calls=%async_computation.1 | async-start | bytes 4194304 | tf_op jit(solution)/shard_map/all_to_all | solution.py:156
  83.4 56.6 %all-gather.1 = f16[2048,1024]{1,0:T(8,128)(2,1)} all-gather(f16[128,1024]{1,0:T(8,128)(2,1)S(1)} %copy-done.8), channel_id=1, replica_groups=mesh['y'=4,'z'=4,'core'=2,'batch'=4] {'y','z'}, dimensions={0}, use_global_device_ids=true | all-gather | bytes 4456448 | tf_op jit(solution)/shard_map/all_gather | solution.py:240
  142.1 3.4 %convert_reduce_fusion = (f32[1024]{0:T(1024)S(1)}, bf16[2048,1024]{1,0:T(8,128)(2,1)S(1)}) fusion(f32[2048]{0:T(1024)S(1)} %fusion.2, f16[2048,1024]{1,0:T(8,128)(2,1)} %all-gather.1, bf16[2048,8]{0,1:T(8,128)(2,1)S(1)} %get-tuple-element.35, bf16[1024,8]{0,1:T(8,128)(2,1)S(1)} %copy-done), kind=kOutput, calls=%fused_computation | convolution fusion | flops 46136320 | bytes 8450048 | tf_op jit(solution)/shard_map/dot_general | solution.py:256
  145.5 1.8 fusion
  150.1 12.5 %all_to_all.22 = f32[32,1,640]{2,1,0:T(1,128)S(1)} all-to-all(f32[32,1,640]{2,1,0:T(1,128)S(1)} %broadcast_in_dim.8), channel_id=1, replica_groups=mesh['y'=4,'z'=4,'core'=2,'batch'=4] {'y','z','core'}, dimensions={0} | all-to-all | bytes 163840 | tf_op jit(solution)/shard_map/all_to_all | solution.py:156
  163.2 2.0 %collective-permute-start.4 = (f32[16,640]{1,0:T(8,128)S(1)}, f32[16,640]{1,0:T(8,128)S(1)}, u32[]{:S(2)}, u32[]{:S(2)}) collective-permute-start(f32[16,640]{1,0:T(8,128)S(1)} %reduce_sum.39), channel_id=1, source_target_pairs={{0,1},{1,2},{2,3},{3,0},{4,5},{5,6},{6,7},{7,4},{8,9},{9,10},{10,1... | collective-permute-start | bytes 122888 | tf_op jit(solution)/shard_map/ppermute | solution.py:161
  165.2 3.0 %collective-permute-start.5 = (f32[16,640]{1,0:T(8,128)S(1)}, f32[16,640]{1,0:T(8,128)S(1)}, u32[]{:S(2)}, u32[]{:S(2)}) collective-permute-start(f32[16,640]{1,0:T(8,128)S(1)} %reduce_sum.39), channel_id=1, source_target_pairs={{0,2},{1,3},{2,0},{3,1},{4,6},{5,7},{6,4},{7,5},{8,10},{9,11},{10,... | collective-permute-start | bytes 122888 | tf_op jit(solution)/shard_map/ppermute | solution.py:161
  168.8 2.0 %collective-permute-done.5 = f32[16,640]{1,0:T(8,128)S(1)} collective-permute-done((f32[16,640]{1,0:T(8,128)S(1)}, f32[16,640]{1,0:T(8,128)S(1)}, u32[]{:S(2)}, u32[]{:S(2)}) %collective-permute-start.5) | collective-permute-done | bytes 40992 | tf_op jit(solution)/shard_map/ppermute | solution.py:161
  172.6 1.2 bitcast_add_fusion
  173.8 1.6 collective-permute-start.3
  175.5 1.6 collective-permute-start.2
  177.0 1.3 collective-permute-start.1
  178.9 2.5 %collective-permute-done.3 = f32[48,1024]{1,0:T(8,128)S(1)} collective-permute-done((f32[48,1024]{1,0:T(8,128)S(1)}, f32[48,1024]{1,0:T(8,128)S(1)}, u32[]{:S(2)}, u32[]{:S(2)}) %collective-permute-start.3) | collective-permute-done | bytes 196640 | tf_op jit(solution)/shard_map/ppermute | solution.py:161
  181.4 2.9 %collective-permute-done.2 = f32[48,1024]{1,0:T(8,128)S(1)} collective-permute-done((f32[48,1024]{1,0:T(8,128)S(1)}, f32[48,1024]{1,0:T(8,128)S(1)}, u32[]{:S(2)}, u32[]{:S(2)}) %collective-permute-start.2) | collective-permute-done | bytes 196640 | tf_op jit(solution)/shard_map/ppermute | solution.py:161
  184.3 2.1 %collective-permute-done.1 = f32[48,1024]{1,0:T(8,128)S(1)} collective-permute-done((f32[48,1024]{1,0:T(8,128)S(1)}, f32[48,1024]{1,0:T(8,128)S(1)}, u32[]{:S(2)}, u32[]{:S(2)}) %collective-permute-start.1) | collective-permute-done | bytes 196640 | tf_op jit(solution)/shard_map/ppermute | solution.py:161
  (72 shorter events, 16.6 us)
Async XLA Ops:
  0.6 21.9 %copy-start = (bf16[1024,8]{0,1:T(8,128)(2,1)S(1)}, bf16[1024,8]{0,1:T(8,128)(2,1)}, u32[]{:S(2)}) copy-start(bf16[1024,8]{0,1:T(8,128)(2,1)} %param.16) | copy-start | bytes 49156
  0.6 1.2 copy-start.1
  1.9 0.9 copy-start.3
  2.8 10.1 %copy-start.2 = (bf16[1,128,4096]{2,1,0:T(8,128)(2,1)S(1)}, bf16[1,128,4096]{2,1,0:T(8,128)(2,1)}, u32[]{:S(2)}) copy-start(bf16[1,128,4096]{2,1,0:T(8,128)(2,1)} %param.9) | copy-start | bytes 3145732
  2.8 10.1 %copy-start.4 = (bf16[1,128,1024]{2,1,0:T(8,128)(2,1)S(1)}, bf16[1,128,1024]{2,1,0:T(8,128)(2,1)}, u32[]{:S(2)}) copy-start(bf16[1,128,1024]{2,1,0:T(8,128)(2,1)} %param.10) | copy-start | bytes 786436
  2.8 10.1 %copy-start.9 = (f32[1024]{0:T(1024)S(1)}, f32[1024]{0:T(1024)}, u32[]{:S(2)}) copy-start(f32[1024]{0:T(1024)} %param.15) | copy-start | bytes 12292
  4.5 37.4 %all-to-all-start = ((bf16[32,2,128,128]{3,2,1,0:T(8,128)(2,1)}), bf16[32,2,128,128]{3,2,1,0:T(8,128)(2,1)S(1)}, u32[]{:S(2)}, u32[]{:S(2)}) async-start(bf16[32,2,128,128]{3,2,1,0:T(8,128)(2,1)} %by_head.1), calls=%async_computation | async-start | bytes 4194304 | tf_op jit(solution)/shard_map/all_to_all | solution.py:156
  12.9 9.6 %copy-start.10 = (f32[8]{0:T(128)S(1)}, f32[8]{0:T(128)}, u32[]{:S(2)}) copy-start(f32[8]{0:T(128)} %param.17) | copy-start | bytes 100
  25.9 2.2 %copy-start.6 = (bf16[128,16,64]{2,0,1:T(8,128)(2,1)S(1)}, bf16[128,16,64]{2,0,1:T(8,128)(2,1)}, u32[]{:S(2)}) copy-start(bf16[128,16,64]{2,0,1:T(8,128)(2,1)} %copy.43) | copy-start | bytes 786436
  27.2 14.6 %copy-start.5 = (s32[1,32]{1,0:T(1,128)S(1)}, s32[1,32]{1,0:T(1,128)}, u32[]{:S(2)}) copy-start(s32[1,32]{1,0:T(1,128)} %param.13) | copy-start | bytes 388
  66.1 17.4 %copy-start.8 = (f16[128,1024]{1,0:T(8,128)(2,1)S(1)}, f16[128,1024]{1,0:T(8,128)(2,1)}, u32[]{:S(2)}) copy-start(f16[128,1024]{1,0:T(8,128)(2,1)} %get-tuple-element.14) | copy-start | bytes 786436
  78.2 62.1 %all-to-all-start.1 = ((bf16[16,128,512]{2,1,0:T(8,128)(2,1)}), bf16[16,128,512]{2,1,0:T(8,128)(2,1)S(1)}, u32[]{:S(2)}, u32[]{:S(2)}) async-start(bf16[16,128,512]{2,1,0:T(8,128)(2,1)} %maximum_bitcast_fusion), calls=%async_computation.1 | async-start | bytes 4194304 | tf_op jit(solution)/shard_map/all_to_all | solution.py:156
  147.3 1.2 copy-start.7
  149.5 23.1 %collective-permute-start = (f32[192,1024]{1,0:T(8,128)}, f32[192,1024]{1,0:T(8,128)S(1)}, u32[]{:S(2)}, u32[]{:S(2)}) collective-permute-start(f32[192,1024]{1,0:T(8,128)} %dynamic-slice_bitcast_fusion), channel_id=1, source_target_pairs={{0,4},{4,0},{1,5},{5,1},{2,6},{6,2},{3,7},{7,3},{8,12},{12,8},{9,1... | collective-permute-start | bytes 2359304 | tf_op jit(solution)/shard_map/ppermute | solution.py:161
  163.0 5.3 %collective-permute-start.6 = (f32[16,640]{1,0:T(8,128)S(1)}, f32[16,640]{1,0:T(8,128)S(1)}, u32[]{:S(2)}, u32[]{:S(2)}) collective-permute-start(f32[16,640]{1,0:T(8,128)S(1)} %reduce_sum.39), channel_id=1, source_target_pairs={{0,3},{1,0},{2,1},{3,2},{4,7},{5,4},{6,5},{7,6},{8,11},{9,8},{10,9... | collective-permute-start | bytes 122888 | tf_op jit(solution)/shard_map/ppermute | solution.py:161
  163.2 5.6 %collective-permute-start.4 = (f32[16,640]{1,0:T(8,128)S(1)}, f32[16,640]{1,0:T(8,128)S(1)}, u32[]{:S(2)}, u32[]{:S(2)}) collective-permute-start(f32[16,640]{1,0:T(8,128)S(1)} %reduce_sum.39), channel_id=1, source_target_pairs={{0,1},{1,2},{2,3},{3,0},{4,5},{5,6},{6,7},{7,4},{8,9},{9,10},{10,1... | collective-permute-start | bytes 122888 | tf_op jit(solution)/shard_map/ppermute | solution.py:161
  165.2 5.5 %collective-permute-start.5 = (f32[16,640]{1,0:T(8,128)S(1)}, f32[16,640]{1,0:T(8,128)S(1)}, u32[]{:S(2)}, u32[]{:S(2)}) collective-permute-start(f32[16,640]{1,0:T(8,128)S(1)} %reduce_sum.39), channel_id=1, source_target_pairs={{0,2},{1,3},{2,0},{3,1},{4,6},{5,7},{6,4},{7,5},{8,10},{9,11},{10,... | collective-permute-start | bytes 122888 | tf_op jit(solution)/shard_map/ppermute | solution.py:161
  173.8 7.6 %collective-permute-start.3 = (f32[48,1024]{1,0:T(8,128)S(1)}, f32[48,1024]{1,0:T(8,128)S(1)}, u32[]{:S(2)}, u32[]{:S(2)}) collective-permute-start(f32[48,1024]{1,0:T(8,128)S(1)} %get-tuple-element.37), channel_id=1, source_target_pairs={{0,3},{1,0},{2,1},{3,2},{4,7},{5,4},{6,5},{7,6},{8,11},{9,8},{10,9... | collective-permute-start | bytes 589832 | tf_op jit(solution)/shard_map/ppermute | solution.py:161
  175.5 8.8 %collective-permute-start.2 = (f32[48,1024]{1,0:T(8,128)S(1)}, f32[48,1024]{1,0:T(8,128)S(1)}, u32[]{:S(2)}, u32[]{:S(2)}) collective-permute-start(f32[48,1024]{1,0:T(8,128)S(1)} %get-tuple-element.38), channel_id=1, source_target_pairs={{0,2},{1,3},{2,0},{3,1},{4,6},{5,7},{6,4},{7,5},{8,10},{9,11},{10,... | collective-permute-start | bytes 589832 | tf_op jit(solution)/shard_map/ppermute | solution.py:161
  177.0 9.4 %collective-permute-start.1 = (f32[48,1024]{1,0:T(8,128)S(1)}, f32[48,1024]{1,0:T(8,128)S(1)}, u32[]{:S(2)}, u32[]{:S(2)}) collective-permute-start(f32[48,1024]{1,0:T(8,128)S(1)} %get-tuple-element.36), channel_id=1, source_target_pairs={{0,1},{1,2},{2,3},{3,0},{4,5},{5,6},{6,7},{7,4},{8,9},{9,10},{10,1... | collective-permute-start | bytes 589832 | tf_op jit(solution)/shard_map/ppermute | solution.py:161

commit v4 on v3

--- a/solution.py
+++ b/solution.py
@@ -63,9 +63,9 @@
             high = jnp.maximum(high, folded(tile, jnp.max))
 
         def score_step(c, high):
+            column_step(c, 1 - slot, weight)
             tile = product(c)
             scores[slot, c] = tile
-            column_step(c, 1 - slot, weight)
             return jnp.maximum(high, folded(tile, jnp.max))
 
         high = lax.fori_loop(0, r * diagonal, score_step, high)
@@ -150,6 +150,7 @@
 SEQ = ("y", "z", "core")
 PLANE = ("y", "z")
 SIDE = 4
+FINER = 2048.0
 
 
 def exchanged(array, axis):
@@ -169,6 +170,31 @@
         part = lax.dynamic_index_in_dim(block, lax.rem(me + by, size), 0, keepdims=False)
         total = total + shifted(part, axis, by)
     return total
+
+
+def beside(i):
+    return i + 1 - 2 * (i % 2)
+
+
+def across(i):
+    return SIDE - 1 - i
+
+
+def swapped(array, other):
+    return lax.ppermute(array, "batch", [(i, other(i)) for i in range(SIDE)])
+
+
+def halved(block, first, second):
+    me = lax.axis_index("batch")
+
+    def two(i):
+        return jnp.stack([lax.dynamic_index_in_dim(block, j, 0, keepdims=False) for j in (i, second(i))])
+
+    return two(me) + swapped(two(first(me)), first)
+
+
+def finished(kept, second):
+    return kept[0] + swapped(kept[1], second)
 
 
 def in_three(array):
@@ -196,7 +222,6 @@
     heads_kv = output_weight.shape[1]
     hidden = output_weight.shape[0]
     head_size = k_rows.shape[1] // heads_kv
-    group = q_rows.shape[1] // k_rows.shape[1]
     total = rows * seq
     order = block_pos[0]
     limit = lengths[0]
@@ -233,16 +258,28 @@
     spread = exchanged(carried, PLANE)
     partial = head_mass(order, lengths, both, 1.0 / math.sqrt(head_size))
 
-    to_cores = jnp.moveaxis(partial.reshape(chips, cores, rows), 1, 0)
-    to_all = jnp.broadcast_to(to_cores[None], (chips, cores, chips, rows)).reshape(seq, chips, rows)
-    slope, to_all = lax.optimization_barrier((slope, to_all))
-    arrived = exchanged(to_all, SEQ)
-    slopes = lax.all_gather(slope, PLANE, axis=0, tiled=True)
-    slopes, arrived = lax.optimization_barrier((slopes, arrived))
-    mass = jnp.sum(arrived.reshape(heads_kv, group, chips * rows), axis=1)
-    labels = jnp.log1p(mass).T
-
-    spread = spread.reshape(chips * rows, width + 2 * part)
+    by_core = partial.reshape(chips, cores, rows)
+    both_heads = lax.dynamic_index_in_dim(by_core, core, 1, keepdims=False)
+    both_heads = both_heads + shifted(lax.dynamic_index_in_dim(by_core, 1 - core, 1, keepdims=False), "core", 1)
+    high = lax.reduce_precision(both_heads, 5, 10)
+    left = (both_heads - high) * FINER
+    middle = lax.reduce_precision(left, 5, 10)
+    low = (left - middle) * FINER
+    carry = jnp.stack([high, middle, low]).astype(jnp.float16).reshape(-1, hidden)
+    taken = carry.shape[0]
+    carry = jnp.pad(carry, ((0, -taken % 16), (0, 0)))
+    arrived = lax.all_gather(jnp.concatenate([slope, carry]), PLANE, axis=0, tiled=False)
+    slopes = arrived.reshape(-1, hidden)
+    padded = rows + carry.shape[0]
+    sums = jnp.sum(
+        arrived[:, rows:].astype(jnp.float32).reshape(heads_kv, chips // heads_kv, carry.shape[0], hidden), axis=1
+    )
+    third = taken // 3
+    mass = sums[:, :third] + (sums[:, third : 2 * third] + sums[:, 2 * third : taken] * (1.0 / FINER)) * (1.0 / FINER)
+    mass = jnp.pad(mass.reshape(heads_kv, chips, rows), ((0, 0), (0, 0), (0, padded - rows)))
+    labels = jnp.log1p(mass.reshape(heads_kv, chips * padded)).T
+
+    spread = jnp.pad(spread, ((0, 0), (0, padded - rows), (0, 0))).reshape(chips * padded, width + 2 * part)
     feats = spread[:, :width]
     acts = spread[:, width : width + part]
     predicted = from_three(spread[:, width + part : width + part + 3 * heads_kv])
@@ -251,6 +288,7 @@
     blocks = lax.dynamic_index_in_dim(order.reshape(chips, cores), core, 1, keepdims=False)
     position = (blocks[:, None] * rows + offsets[None, :]).reshape(-1)
     live = (position < limit).astype(jnp.float32)
+    live = jnp.pad(live.reshape(chips, rows), ((0, 0), (0, padded - rows))).reshape(-1)
     norm = 1.0 / math.sqrt(batch * total)
     resid = ((predicted - labels) * live[:, None] * norm).astype(jnp.bfloat16)
     back = lax.dot_general(
@@ -269,7 +307,10 @@
         feats, delta, (((0,), (0,)), ((), ())), preferred_element_type=jnp.float32
     )
     block = summed(block.reshape(cores, width // cores, hidden), "core")
-    grad_w_in = summed(block.reshape(batch, width // (cores * batch), hidden), "batch")
+    block = block.reshape(batch, width // (cores * batch), hidden)
+    half = hidden // 2
+    kept = [halved(block[:, :, :half], beside, across), halved(block[:, :, half:], across, beside)]
+    grad_w_in = jnp.concatenate([finished(kept[0], across), finished(kept[1], beside)], axis=1)
     small = jnp.sum(small.reshape(chips, cores, small.shape[1]), axis=1)
     small = small + sum(shifted(small, "batch", by) for by in range(1, batch))
     output_weight_gradient = small[:, : part * heads_kv].reshape(hidden, heads_kv)

time: 188 us -> 180 us (0.957)
  blocking collectives: 81.2 us -> 71.4 us
  local copies, waits for them, and re-layouts: 12.4 us -> 15.5 us
  waiting for transfers between devices: 22 us -> 19.4 us
    all_to_all x2 -> x1, blocking collectives: 24.6 us -> 12.4 us  [exchanged(): return lax.all_to_all(array, axis, 0, 0, tiled=True)]
    ppermute x0 -> x4, waiting for transfers between devices: none -> 8.91 us  [swapped(): return lax.ppermute(array, 'batch', [(i, other(i)) for i in range(SIDE)])]
    ppermute x7 -> x5, waiting for transfers between devices: 9.95 us -> 2.49 us  [shifted(): lax.ppermute(array, axis, [(i, (i + by) % size) for i in range(size)])]
    ppermute x0 -> x4, starting transfers between devices: none -> 4.91 us  [swapped(): return lax.ppermute(array, 'batch', [(i, other(i)) for i in range(SIDE)])]
    ppermute x7 -> x5, starting transfers between devices: 9.82 us -> 5.19 us  [shifted(): lax.ppermute(array, axis, [(i, (i + by) % size) for i in range(size)])]
    all_to_all x2, waiting for transfers between devices: 12.1 us -> 8.02 us  [exchanged(): return lax.all_to_all(array, axis, 0, 0, tiled=True)]
    all_gather x1, blocking collectives: 56.6 us -> 59 us  [on_device(): lax.all_gather(jnp.concatenate([slope, carry]), PLANE, axis=0, tiled=False)]
    unnamed x26 -> x31, local copies, waits for them, and re-layouts: 5 us -> 6.3 us
  transfers between devices with their start and end apart: 9 -> 11, of which waited for: 6 -> 6; matrix products, arithmetic and copies ran while one was open for 11% -> 14% of each run, Pallas kernels for 0% -> 0%
where the time goes in v4:
time: 180 us; the launch traced here: 179 us
  blocking collectives  71.4 us (40%)
  Pallas kernels  24.9 us (14%)
  starting transfers between devices  22.5 us (12%)
  waiting for transfers between devices  19.4 us (11%)
  local copies, waits for them, and re-layouts  15.5 us (9%)
  matrix products  13.2 us (7%)
  other arithmetic  10.4 us (6%)
  between operations  1.81 us (1%)
    all_gather x1, blocking collectives, on_device(): lax.all_gather(jnp.concatenate([slope, carry]), PLANE, axis=0, tiled=False)  59 us
    pallas_call x1, Pallas kernels, head_mass(): pl.pallas_call(functools.partial(mass_kernel, scale=scale), out_shape=jax...  23.3 us
    all_to_all x2, starting transfers between devices, exchanged(): return lax.all_to_all(array, axis, 0, 0, tiled=True)  12.4 us
    all_to_all x1, blocking collectives, exchanged(): return lax.all_to_all(array, axis, 0, 0, tiled=True)  12.4 us
    ppermute x4, waiting for transfers between devices, swapped(): return lax.ppermute(array, 'batch', [(i, other(i)) for i in range(SIDE)])  8.91 us
    all_to_all x2, waiting for transfers between devices, exchanged(): return lax.all_to_all(array, axis, 0, 0, tiled=True)  8.02 us
    dot_general x1, matrix products, on_device(): pre = jnp.dot(features, w_in, preferred_element_type=jnp.float32) + b_in  6.68 us
    unnamed x31, local copies, waits for them, and re-layouts  6.3 us
  transfers between devices with their start and end apart: 11, of which 6 were waited for; matrix products, arithmetic and copies ran while one was open for 14% of the time, Pallas kernels for 0%

profile of v4, /device:TPU:0, one launch (start us, length us, event | category | flops | bytes accessed | tf_op | source)
XLA Modules:
  0.0 179.2 jit_solution(10157547693550061815)
XLA Ops:
  2.8 1.6 by_head.1
  4.5 8.6 %all-to-all-start = ((bf16[32,2,128,128]{3,2,1,0:T(8,128)(2,1)}), bf16[32,2,128,128]{3,2,1,0:T(8,128)(2,1)S(1)}, u32[]{:S(2)}, u32[]{:S(2)}) async-start(bf16[32,2,128,128]{3,2,1,0:T(8,128)(2,1)} %by_head.1), calls=%async_computation | async-start | bytes 4194304 | tf_op jit(solution)/shard_map/all_to_all | solution.py:157
  13.1 6.7 %abs_reduce_fusion = (f32[128]{0:T(128)S(1)}, f32[128,1024]{1,0:T(8,128)S(1)}) fusion(f32[1024]{0:T(1024)S(1)} %copy-done.10, bf16[6144,1024]{1,0:T(8,128)(2,1)} %param.14, bf16[128,1024]{1,0:T(8,128)(2,1)} %bitcast.92, bf16[128,1024]{1,0:T(8,128)(2,1)S(1)} %bitcast.75, bf16[128,4096]{1,0:T(8,128)(2,1)S(1)} %bitcast.72), kind=kOutput, calls=%fused_computation.32 | convolution fusion | flops 1616641920 | bytes 14684672 | tf_op jit(solution)/shard_map/dot_general | solution.py:234
  20.8 1.8 copy.42
  24.0 2.0 %copy.45 = bf16[128,16,64]{2,0,1:T(8,128)(2,1)} copy(bf16[128,16,64]{0,2,1:T(8,128)(2,1)} %bitcast.91) | data formatting | bytes 524288 | tf_op jit(solution)/shard_map/reshape | solution.py:247
  27.0 1.4 copy.56
  30.7 3.2 %maximum_bitcast_fusion = bf16[16,128,512]{2,1,0:T(8,128)(2,1)} fusion(bf16[128,16,64]{2,0,1:T(8,128)(2,1)S(1)} %broadcast_in_dim.4, bf16[128,16,64]{2,0,1:T(8,128)(2,1)S(1)} %copy-done.8, bf16[128,16,384]{2,0,1:T(8,128)(2,1)} %bitcast.84), kind=kLoop, calls=%fused_computation.4 | loop fusion | flops 6291456 | bytes 4194304 | tf_op jit(solution)/shard_map/transpose | solution.py:257
  34.0 8.0 %all-to-all-done.both_ref = bf16[32,2,128,128]{3,2,1,0:T(8,128)(2,1)S(1)} async-done(((bf16[32,2,128,128]{3,2,1,0:T(8,128)(2,1)}), bf16[32,2,128,128]{3,2,1,0:T(8,128)(2,1)S(1)}, u32[]{:S(2)}, u32[]{:S(2)}) %all-to-all-start) | async-done | bytes 2097184 | tf_op jit(solution)/shard_map/all_to_all | solution.py:157
  42.0 23.3 %head_mass.1 = f32[32,128]{1,0:T(8,128)S(1)} custom-call(s32[32]{0:T(128)S(1)} %bitcast.78, s32[1]{0:T(128)} %copy.57.limit_ref, bf16[32,2,128,128]{3,2,1,0:T(8,128)(2,1)S(1)} %all-to-all-done.both_ref), custom_call_target="tpu_custom_call" | custom-call | flops 4294967296 | bytes 2097152 | tf_op jit(solution)/shard_map/head_mass/pallas_call | solution.py:109
  65.5 3.9 %all-to-all-start.1 = ((bf16[16,128,512]{2,1,0:T(8,128)(2,1)}), bf16[16,128,512]{2,1,0:T(8,128)(2,1)S(1)}, u32[]{:S(2)}, u32[]{:S(2)}) async-start(bf16[16,128,512]{2,1,0:T(8,128)(2,1)} %maximum_bitcast_fusion), calls=%async_computation.1 | async-start | bytes 4194304 | tf_op jit(solution)/shard_map/all_to_all | solution.py:157
  69.6 59.0 %all-gather.2 = f16[2304,1024]{1,0:T(8,128)(2,1)S(1)} all-gather(f16[144,1024]{1,0:T(8,128)(2,1)S(1)} %fusion.12), channel_id=2, replica_groups=mesh['y'=4,'z'=4,'core'=2,'batch'=4] {'y','z'}, dimensions={0}, use_global_device_ids=true | all-gather | bytes 5013504 | tf_op jit(solution)/shard_map/all_gather | solution.py:271
  128.5 2.1 %copy-done.7 = f16[2304,1024]{1,0:T(8,128)(2,1)} copy-done((f16[2304,1024]{1,0:T(8,128)(2,1)}, f16[2304,1024]{1,0:T(8,128)(2,1)S(1)}, u32[]{:S(2)}) %copy-start.7) | copy-done | bytes 4718616
  134.8 2.1 %convert_reduce_fusion = (f32[1024]{0:T(1024)S(1)}, bf16[2304,1024]{1,0:T(8,128)(2,1)S(1)}) fusion(f32[2304]{0:T(1024)S(1)} %fusion.4, f16[2304,1024]{1,0:T(8,128)(2,1)S(1)} %bitcast.87, bf16[2304,8]{1,0:T(8,128)(2,1)S(1)} %get-tuple-element.31, bf16[1024,8]{0,1:T(8,128)(2,1)S(1)} %copy-done), kind=kOutput, calls=%fused_computation.3 | convolution fusion | flops 51903488 | bytes 9503744 | tf_op jit(solution)/shard_map/dot_general | solution.py:294
  136.8 2.0 %fusion.2 = f32[384,1024]{1,0:T(8,128)S(1)} fusion(bf16[2304,1024]{1,0:T(8,128)(2,1)S(1)} %get-tuple-element.58, bf16[2304,512]{1,0:T(8,128)(2,1)S(1)} %bitcast.81), kind=kOutput, calls=%fused_computation.5 | convolution fusion | flops 1811939328 | bytes 8060928 | tf_op jit(solution)/shard_map/dot_general | solution.py:306
  141.5 12.4 %all_to_all.16 = f32[32,1,640]{2,1,0:T(1,128)S(1)} all-to-all(f32[32,1,640]{2,1,0:T(1,128)S(1)} %broadcast_in_dim.5), channel_id=1, replica_groups=mesh['y'=4,'z'=4,'core'=2,'batch'=4] {'y','z','core'}, dimensions={0} | all-to-all | bytes 163840 | tf_op jit(solution)/shard_map/all_to_all | solution.py:157
  154.4 2.0 %collective-permute-start.6 = (f32[16,640]{1,0:T(8,128)S(1)}, f32[16,640]{1,0:T(8,128)S(1)}, u32[]{:S(2)}, u32[]{:S(2)}) collective-permute-start(f32[16,640]{1,0:T(8,128)S(1)} %reduce_sum.39), channel_id=1, source_target_pairs={{0,1},{1,2},{2,3},{3,0},{4,5},{5,6},{6,7},{7,4},{8,9},{9,10},{10,1... | collective-permute-start | bytes 122888 | tf_op jit(solution)/shard_map/ppermute | solution.py:162
  156.4 3.0 %collective-permute-start.7 = (f32[16,640]{1,0:T(8,128)S(1)}, f32[16,640]{1,0:T(8,128)S(1)}, u32[]{:S(2)}, u32[]{:S(2)}) collective-permute-start(f32[16,640]{1,0:T(8,128)S(1)} %reduce_sum.39), channel_id=1, source_target_pairs={{0,2},{1,3},{2,0},{3,1},{4,6},{5,7},{6,4},{7,5},{8,10},{9,11},{10,... | collective-permute-start | bytes 122888 | tf_op jit(solution)/shard_map/ppermute | solution.py:162
  159.9 2.0 %collective-permute-done.7 = f32[16,640]{1,0:T(8,128)S(1)} collective-permute-done((f32[16,640]{1,0:T(8,128)S(1)}, f32[16,640]{1,0:T(8,128)S(1)}, u32[]{:S(2)}, u32[]{:S(2)}) %collective-permute-start.7) | collective-permute-done | bytes 40992 | tf_op jit(solution)/shard_map/ppermute | solution.py:162
  162.2 1.6 collective-permute-start.4
  166.2 1.5 collective-permute-start.2
  167.7 1.5 collective-permute-done.4
  169.3 3.3 %collective-permute-done.2 = f32[2,48,512]{2,1,0:T(8,128)S(1)} collective-permute-done((f32[2,48,512]{2,1,0:T(8,128)S(1)}, f32[2,48,512]{2,1,0:T(8,128)S(1)}, u32[]{:S(2)}, u32[]{:S(2)}) %collective-permute-start.2) | collective-permute-done | bytes 196640 | tf_op jit(solution)/shard_map/ppermute | solution.py:184
  172.6 1.7 collective-permute-start.3
  174.3 4.2 %collective-permute-done.3 = f32[48,512]{1,0:T(8,128)S(1)} collective-permute-done((f32[48,512]{1,0:T(8,128)S(1)}, f32[48,512]{1,0:T(8,128)S(1)}, u32[]{:S(2)}, u32[]{:S(2)}) %collective-permute-start.3) | collective-permute-done | bytes 98336 | tf_op jit(solution)/shard_map/ppermute | solution.py:184
  (98 shorter events, 18.7 us)
Async XLA Ops:
  0.6 22.0 %copy-start = (bf16[1024,8]{0,1:T(8,128)(2,1)S(1)}, bf16[1024,8]{0,1:T(8,128)(2,1)}, u32[]{:S(2)}) copy-start(bf16[1024,8]{0,1:T(8,128)(2,1)} %param.16) | copy-start | bytes 49156
  0.6 1.2 copy-start.1
  4.5 8.6 %copy-start.2 = (bf16[1,128,4096]{2,1,0:T(8,128)(2,1)S(1)}, bf16[1,128,4096]{2,1,0:T(8,128)(2,1)}, u32[]{:S(2)}) copy-start(bf16[1,128,4096]{2,1,0:T(8,128)(2,1)} %param.9) | copy-start | bytes 3145732
  4.5 8.6 %copy-start.4 = (bf16[1,128,1024]{2,1,0:T(8,128)(2,1)S(1)}, bf16[1,128,1024]{2,1,0:T(8,128)(2,1)}, u32[]{:S(2)}) copy-start(bf16[1,128,1024]{2,1,0:T(8,128)(2,1)} %param.10) | copy-start | bytes 786436
  4.5 8.6 %copy-start.10 = (f32[1024]{0:T(1024)S(1)}, f32[1024]{0:T(1024)}, u32[]{:S(2)}) copy-start(f32[1024]{0:T(1024)} %param.15) | copy-start | bytes 12292
  4.5 37.5 %all-to-all-start = ((bf16[32,2,128,128]{3,2,1,0:T(8,128)(2,1)}), bf16[32,2,128,128]{3,2,1,0:T(8,128)(2,1)S(1)}, u32[]{:S(2)}, u32[]{:S(2)}) async-start(bf16[32,2,128,128]{3,2,1,0:T(8,128)(2,1)} %by_head.1), calls=%async_computation | async-start | bytes 4194304 | tf_op jit(solution)/shard_map/all_to_all | solution.py:157
  13.1 9.5 %copy-start.11 = (f32[8]{0:T(128)S(1)}, f32[8]{0:T(128)}, u32[]{:S(2)}) copy-start(f32[8]{0:T(128)} %param.17) | copy-start | bytes 100
  27.0 2.6 %copy-start.5 = (s32[1,32]{1,0:T(1,128)S(1)}, s32[1,32]{1,0:T(1,128)}, u32[]{:S(2)}) copy-start(s32[1,32]{1,0:T(1,128)} %param.13) | copy-start | bytes 388
  27.0 3.7 %copy-start.8 = (bf16[128,16,64]{2,0,1:T(8,128)(2,1)S(1)}, bf16[128,16,64]{2,0,1:T(8,128)(2,1)}, u32[]{:S(2)}) copy-start(bf16[128,16,64]{2,0,1:T(8,128)(2,1)} %copy.45) | copy-start | bytes 786436
  65.3 4.1 %collective-permute-start = (f32[16,128]{1,0:T(8,128)S(1)}, f32[16,128]{1,0:T(8,128)S(1)}, u32[]{:S(2)}, u32[]{:S(2)}) collective-permute-start(f32[16,128]{1,0:T(8,128)S(1)} %bitcast.95), channel_id=1, source_target_pairs={{0,4},{4,0},{1,5},{5,1},{2,6},{6,2},{3,7},{7,3},{8,12},{12,8},{9,1... | collective-permute-start | bytes 24584 | tf_op jit(solution)/shard_map/ppermute | solution.py:162
  65.5 4.0 %copy-start.9 = (f16[128,1024]{1,0:T(8,128)(2,1)S(1)}, f16[128,1024]{1,0:T(8,128)(2,1)}, u32[]{:S(2)}) copy-start(f16[128,1024]{1,0:T(8,128)(2,1)} %get-tuple-element.8) | copy-start | bytes 786436
  65.5 65.9 %all-to-all-start.1 = ((bf16[16,128,512]{2,1,0:T(8,128)(2,1)}), bf16[16,128,512]{2,1,0:T(8,128)(2,1)S(1)}, u32[]{:S(2)}, u32[]{:S(2)}) async-start(bf16[16,128,512]{2,1,0:T(8,128)(2,1)} %maximum_bitcast_fusion), calls=%async_computation.1 | async-start | bytes 4194304 | tf_op jit(solution)/shard_map/all_to_all | solution.py:157
  128.5 2.1 %copy-start.7 = (f16[2304,1024]{1,0:T(8,128)(2,1)}, f16[2304,1024]{1,0:T(8,128)(2,1)S(1)}, u32[]{:S(2)}) copy-start(f16[2304,1024]{1,0:T(8,128)(2,1)S(1)} %all-gather.2) | copy-start | bytes 14155780
  131.6 5.2 %copy-start.6 = (bf16[16,144,512]{2,1,0:T(8,128)(2,1)}, bf16[16,144,512]{2,1,0:T(8,128)(2,1)S(1)}, u32[]{:S(2)}) copy-start(bf16[16,144,512]{2,1,0:T(8,128)(2,1)S(1)} %pad.26) | copy-start | bytes 7077892
  131.6 3.0 %slice-start = ((s8[4718592]{0:T(1024)(128)(4,1)}), s8[4194304]{0:T(1024)(128)(4,1)S(1)}, s32[]{:S(2)}) async-start(s8[4718592]{0:T(1024)(128)(4,1)} %bitcast.86), calls=%async_computation.3 | async-start | bytes 8388608
  132.1 2.7 %slice-start.1 = ((s8[4718592]{0:T(1024)(128)(4,1)}), s8[524288]{0:T(1024)(128)(4,1)S(1)}, s32[]{:S(2)}) async-start(s8[4718592]{0:T(1024)(128)(4,1)} %bitcast.86), calls=%async_computation.4 | async-start | bytes 1048576
  139.8 22.1 %collective-permute-start.1 = (f32[192,1024]{1,0:T(8,128)}, f32[192,1024]{1,0:T(8,128)S(1)}, u32[]{:S(2)}, u32[]{:S(2)}) collective-permute-start(f32[192,1024]{1,0:T(8,128)} %dynamic-slice_bitcast_fusion), channel_id=1, source_target_pairs={{0,4},{4,0},{1,5},{5,1},{2,6},{6,2},{3,7},{7,3},{8,12},{12,8},{9,1... | collective-permute-start | bytes 2359304 | tf_op jit(solution)/shard_map/ppermute | solution.py:162
  154.3 5.1 %collective-permute-start.8 = (f32[16,640]{1,0:T(8,128)S(1)}, f32[16,640]{1,0:T(8,128)S(1)}, u32[]{:S(2)}, u32[]{:S(2)}) collective-permute-start(f32[16,640]{1,0:T(8,128)S(1)} %reduce_sum.39), channel_id=1, source_target_pairs={{0,3},{1,0},{2,1},{3,2},{4,7},{5,4},{6,5},{7,6},{8,11},{9,8},{10,9... | collective-permute-start | bytes 122888 | tf_op jit(solution)/shard_map/ppermute | solution.py:162
  154.4 5.5 %collective-permute-start.6 = (f32[16,640]{1,0:T(8,128)S(1)}, f32[16,640]{1,0:T(8,128)S(1)}, u32[]{:S(2)}, u32[]{:S(2)}) collective-permute-start(f32[16,640]{1,0:T(8,128)S(1)} %reduce_sum.39), channel_id=1, source_target_pairs={{0,1},{1,2},{2,3},{3,0},{4,5},{5,6},{6,7},{7,4},{8,9},{9,10},{10,1... | collective-permute-start | bytes 122888 | tf_op jit(solution)/shard_map/ppermute | solution.py:162
  156.4 5.5 %collective-permute-start.7 = (f32[16,640]{1,0:T(8,128)S(1)}, f32[16,640]{1,0:T(8,128)S(1)}, u32[]{:S(2)}, u32[]{:S(2)}) collective-permute-start(f32[16,640]{1,0:T(8,128)S(1)} %reduce_sum.39), channel_id=1, source_target_pairs={{0,2},{1,3},{2,0},{3,1},{4,6},{5,7},{6,4},{7,5},{8,10},{9,11},{10,... | collective-permute-start | bytes 122888 | tf_op jit(solution)/shard_map/ppermute | solution.py:162
  162.2 7.0 %collective-permute-start.4 = (f32[2,48,512]{2,1,0:T(8,128)S(1)}, f32[2,48,512]{2,1,0:T(8,128)S(1)}, u32[]{:S(2)}, u32[]{:S(2)}) collective-permute-start(f32[2,48,512]{2,1,0:T(8,128)S(1)} %pad_maximum_fusion.2), channel_id=1, source_target_pairs={{0,3},{1,2},{2,1},{3,0},{4,7},{5,6},{6,5},{7,4},{8,11},{9,10},{10,... | collective-permute-start | bytes 589832 | tf_op jit(solution)/shard_map/ppermute | solution.py:184
  166.2 6.3 %collective-permute-start.2 = (f32[2,48,512]{2,1,0:T(8,128)S(1)}, f32[2,48,512]{2,1,0:T(8,128)S(1)}, u32[]{:S(2)}, u32[]{:S(2)}) collective-permute-start(f32[2,48,512]{2,1,0:T(8,128)S(1)} %pad_maximum_fusion.1), channel_id=1, source_target_pairs={{0,1},{1,0},{2,3},{3,2},{4,5},{5,4},{6,7},{7,6},{8,9},{9,8},{10,11... | collective-permute-start | bytes 589832 | tf_op jit(solution)/shard_map/ppermute | solution.py:184
  169.2 5.1 %collective-permute-start.5 = (f32[48,512]{1,0:T(8,128)S(1)}, f32[48,512]{1,0:T(8,128)S(1)}, u32[]{:S(2)}, u32[]{:S(2)}) collective-permute-start(f32[48,512]{1,0:T(8,128)S(1)} %slice_bitcast_fusion), channel_id=1, source_target_pairs={{0,1},{1,0},{2,3},{3,2},{4,5},{5,4},{6,7},{7,6},{8,9},{9,8},{10,11... | collective-permute-start | bytes 294920 | tf_op jit(solution)/shard_map/ppermute | solution.py:184
  172.6 5.9 %collective-permute-start.3 = (f32[48,512]{1,0:T(8,128)S(1)}, f32[48,512]{1,0:T(8,128)S(1)}, u32[]{:S(2)}, u32[]{:S(2)}) collective-permute-start(f32[48,512]{1,0:T(8,128)S(1)} %slice_bitcast_fusion.2), channel_id=1, source_target_pairs={{0,3},{1,2},{2,1},{3,0},{4,7},{5,6},{6,5},{7,4},{8,11},{9,10},{10,... | collective-permute-start | bytes 294920 | tf_op jit(solution)/shard_map/ppermute | solution.py:184
  (1 other events, 0.9 us)

commit v5 on v4

--- a/solution.py
+++ b/solution.py
@@ -14,7 +14,7 @@
 KEYS = 512
 
 
-def mass_kernel(order_ref, limit_ref, both_ref, out_ref, where_ref, keys, scores, col, *, scale):
+def mass_kernel(order_ref, limit_ref, both_ref, out_ref, where_ref, keys, even, odd, col, *, scale):
     blocks = both_ref.shape[0]
     limit = limit_ref[0]
     factor = scale * math.log2(math.e)
@@ -35,17 +35,33 @@
     def folded(tile, op):
         return op(tile.reshape(KEYS // 8, 8, QUERIES), axis=0)
 
-    def column_step(c, slot, weight):
-        tile = scores[slot, c] * weight
+    def column_step(c, scores, weight):
+        tile = scores[c] * weight
         part = tile[:, :BLOCK]
         for i in range(1, lanes):
             part = part + tile[:, i * BLOCK : (i + 1) * BLOCK]
         col[c] += part
 
-    def query_block(r, weight):
+    def columns(scores, weight, r):
+        def one(c, carry):
+            column_step(c, scores, weight)
+            return carry
+
+        lax.fori_loop(0, r * diagonal, one, 0)
+
+    def exponents(c, scores, top):
+        tile = jnp.exp2(scores[c] - top)
+        scores[c] = tile
+        return folded(tile, jnp.sum)
+
+    def weights(sums, r):
+        total = jnp.sum(sums, axis=0, keepdims=True)
+        live = lax.broadcasted_iota(jnp.int32, (1, QUERIES), 1) + r * QUERIES < limit
+        return jnp.where(live & (total > 0.0), 1.0 / total, 0.0)
+
+    def query_block(r, top, scores, earlier):
         parts = [both_ref[where_ref[r * lanes + i], 0] for i in range(lanes)]
         q_rows = jnp.concatenate(parts, axis=0)
-        slot = lax.rem(r, 2)
 
         def product(c):
             k_rows = keys[pl.ds(pl.multiple_of(c * KEYS, KEYS), KEYS), :]
@@ -59,37 +75,32 @@
             c = r * diagonal + d
             allowed = (key + d * KEYS <= query) & (key + c * KEYS < limit)
             tile = jnp.where(allowed, product(c), -1e30)
-            scores[slot, c] = tile
+            scores[c] = tile
             high = jnp.maximum(high, folded(tile, jnp.max))
 
-        def score_step(c, high):
-            column_step(c, 1 - slot, weight)
+        def step(c, carry):
+            high, sums = carry
             tile = product(c)
-            scores[slot, c] = tile
-            return jnp.maximum(high, folded(tile, jnp.max))
-
-        high = lax.fori_loop(0, r * diagonal, score_step, high)
-        top = jnp.max(high, axis=0, keepdims=True)
-
-        def exp_step(c, sums):
-            tile = jnp.exp2(scores[slot, c] - top)
-            scores[slot, c] = tile
-            return sums + folded(tile, jnp.sum)
-
-        sums = lax.fori_loop(0, (r + 1) * diagonal, exp_step, jnp.zeros((8, QUERIES), jnp.float32))
-        total = jnp.sum(sums, axis=0, keepdims=True)
-        live = lax.broadcasted_iota(jnp.int32, (1, QUERIES), 1) + r * QUERIES < limit
-        return jnp.where(live, 1.0 / total, 0.0)
-
-    count = (limit + QUERIES - 1) // QUERIES
-    weight = lax.fori_loop(0, count, query_block, jnp.zeros((1, QUERIES), jnp.float32))
-    last = lax.rem(count - 1, 2)
-
-    def last_step(c, carry):
-        column_step(c, last, weight)
-        return carry
-
-    lax.fori_loop(0, count * diagonal, last_step, 0)
+            scores[c] = tile
+            sums = sums + exponents(c, earlier, top)
+            return jnp.maximum(high, folded(tile, jnp.max)), sums
+
+        high, sums = lax.fori_loop(0, r * diagonal, step, (high, jnp.zeros((8, QUERIES), jnp.float32)))
+        columns(earlier, weights(sums, r - 1), r)
+        return jnp.max(high, axis=0, keepdims=True)
+
+    def query_pair(i, top):
+        top = query_block(2 * i, top, even, odd)
+        return query_block(2 * i + 1, top, odd, even)
+
+    pairs = (limit + 2 * QUERIES - 1) // (2 * QUERIES)
+    top = lax.fori_loop(0, pairs, query_pair, jnp.zeros((1, QUERIES), jnp.float32))
+
+    def last_step(c, sums):
+        return sums + exponents(c, odd, top)
+
+    sums = lax.fori_loop(0, 2 * pairs * diagonal, last_step, jnp.zeros((8, QUERIES), jnp.float32))
+    columns(odd, weights(sums, 2 * pairs - 1), 2 * pairs)
 
     def store(i, carry):
         p = order_ref[i]
@@ -114,7 +125,8 @@
         scratch_shapes=[
             pltpu.SMEM((blocks,), jnp.int32),
             pltpu.VMEM((tokens, size), jnp.bfloat16),
-            pltpu.VMEM((2, tokens // KEYS, KEYS, QUERIES), jnp.float32),
+            pltpu.VMEM((tokens // KEYS, KEYS, QUERIES), jnp.float32),
+            pltpu.VMEM((tokens // KEYS, KEYS, QUERIES), jnp.float32),
             pltpu.VMEM((tokens // KEYS, KEYS, BLOCK), jnp.float32),
         ],
         compiler_params=pltpu.CompilerParams(vmem_limit_bytes=48 * 1024 * 1024),

time: 180 us -> 177 us (0.983)
  Pallas kernels: 24.9 us -> 21.7 us
    pallas_call x1, Pallas kernels: 23.3 us -> 20.1 us  [head_mass(): pl.pallas_call(functools.partial(mass_kernel, scale=scale), out_shape=jax...]
where the time goes in v5:
time: 177 us; the launch traced here: 176 us
  blocking collectives  71.4 us (40%)
  starting transfers between devices  22.5 us (13%)
  Pallas kernels  21.7 us (12%)
  waiting for transfers between devices  19.4 us (11%)
  local copies, waits for them, and re-layouts  15.5 us (9%)
  matrix products  13.2 us (7%)
  other arithmetic  10.4 us (6%)
  between operations  1.81 us (1%)
    all_gather x1, blocking collectives, on_device(): lax.all_gather(jnp.concatenate([slope, carry]), PLANE, axis=0, tiled=False)  59 us
    pallas_call x1, Pallas kernels, head_mass(): pl.pallas_call(functools.partial(mass_kernel, scale=scale), out_shape=jax...  20.1 us
    all_to_all x2, starting transfers between devices, exchanged(): return lax.all_to_all(array, axis, 0, 0, tiled=True)  12.4 us
    all_to_all x1, blocking collectives, exchanged(): return lax.all_to_all(array, axis, 0, 0, tiled=True)  12.4 us
    ppermute x4, waiting for transfers between devices, swapped(): return lax.ppermute(array, 'batch', [(i, other(i)) for i in range(SIDE)])  8.91 us
    all_to_all x2, waiting for transfers between devices, exchanged(): return lax.all_to_all(array, axis, 0, 0, tiled=True)  8.02 us
    dot_general x1, matrix products, on_device(): pre = jnp.dot(features, w_in, preferred_element_type=jnp.float32) + b_in  6.68 us
    unnamed x31, local copies, waits for them, and re-layouts  6.3 us
  transfers between devices with their start and end apart: 11, of which 6 were waited for; matrix products, arithmetic and copies ran while one was open for 14% of the time, Pallas kernels for 0%

profile of v5, /device:TPU:0, one launch (start us, length us, event | category | flops | bytes accessed | tf_op | source)
XLA Modules:
  0.0 176.0 jit_solution(16577945163896034848)
XLA Ops:
  2.8 1.6 by_head.1
  4.5 8.6 %all-to-all-start = ((bf16[32,2,128,128]{3,2,1,0:T(8,128)(2,1)}), bf16[32,2,128,128]{3,2,1,0:T(8,128)(2,1)S(1)}, u32[]{:S(2)}, u32[]{:S(2)}) async-start(bf16[32,2,128,128]{3,2,1,0:T(8,128)(2,1)} %by_head.1), calls=%async_computation | async-start | bytes 4194304 | tf_op jit(solution)/shard_map/all_to_all | solution.py:169
  13.1 6.7 %abs_reduce_fusion = (f32[128]{0:T(128)S(1)}, f32[128,1024]{1,0:T(8,128)S(1)}) fusion(f32[1024]{0:T(1024)S(1)} %copy-done.10, bf16[6144,1024]{1,0:T(8,128)(2,1)} %param.14, bf16[128,1024]{1,0:T(8,128)(2,1)} %bitcast.92, bf16[128,1024]{1,0:T(8,128)(2,1)S(1)} %bitcast.75, bf16[128,4096]{1,0:T(8,128)(2,1)S(1)} %bitcast.72), kind=kOutput, calls=%fused_computation.32 | convolution fusion | flops 1616641920 | bytes 14684672 | tf_op jit(solution)/shard_map/dot_general | solution.py:246
  20.8 1.8 %copy.42 = bf16[128,1024]{0,1:T(8,128)(2,1)} copy(bf16[128,1024]{1,0:T(8,128)(2,1)} %get-tuple-element.34) | data formatting | bytes 524288 | tf_op jit(solution)/shard_map/convert_element_type | solution.py:248
  24.0 2.0 %copy.45 = bf16[128,16,64]{2,0,1:T(8,128)(2,1)} copy(bf16[128,16,64]{0,2,1:T(8,128)(2,1)} %bitcast.91) | data formatting | bytes 524288 | tf_op jit(solution)/shard_map/reshape | solution.py:259
  27.0 1.4 copy.56
  30.7 3.2 %maximum_bitcast_fusion = bf16[16,128,512]{2,1,0:T(8,128)(2,1)} fusion(bf16[128,16,64]{2,0,1:T(8,128)(2,1)S(1)} %broadcast_in_dim.4, bf16[128,16,64]{2,0,1:T(8,128)(2,1)S(1)} %copy-done.8, bf16[128,16,384]{2,0,1:T(8,128)(2,1)} %bitcast.84), kind=kLoop, calls=%fused_computation.4 | loop fusion | flops 6291456 | bytes 4194304 | tf_op jit(solution)/shard_map/transpose | solution.py:269
  34.0 8.0 %all-to-all-done.both_ref = bf16[32,2,128,128]{3,2,1,0:T(8,128)(2,1)S(1)} async-done(((bf16[32,2,128,128]{3,2,1,0:T(8,128)(2,1)}), bf16[32,2,128,128]{3,2,1,0:T(8,128)(2,1)S(1)}, u32[]{:S(2)}, u32[]{:S(2)}) %all-to-all-start) | async-done | bytes 2097184 | tf_op jit(solution)/shard_map/all_to_all | solution.py:169
  42.0 20.1 %head_mass.1 = f32[32,128]{1,0:T(8,128)S(1)} custom-call(s32[32]{0:T(128)S(1)} %bitcast.78, s32[1]{0:T(128)} %copy.57.limit_ref, bf16[32,2,128,128]{3,2,1,0:T(8,128)(2,1)S(1)} %all-to-all-done.both_ref), custom_call_target="tpu_custom_call" | custom-call | flops 4294967296 | bytes 2097152 | tf_op jit(solution)/shard_map/head_mass/pallas_call | solution.py:120
  62.3 3.9 %all-to-all-start.1 = ((bf16[16,128,512]{2,1,0:T(8,128)(2,1)}), bf16[16,128,512]{2,1,0:T(8,128)(2,1)S(1)}, u32[]{:S(2)}, u32[]{:S(2)}) async-start(bf16[16,128,512]{2,1,0:T(8,128)(2,1)} %maximum_bitcast_fusion), calls=%async_computation.1 | async-start | bytes 4194304 | tf_op jit(solution)/shard_map/all_to_all | solution.py:169
  66.3 59.0 %all-gather.2 = f16[2304,1024]{1,0:T(8,128)(2,1)S(1)} all-gather(f16[144,1024]{1,0:T(8,128)(2,1)S(1)} %fusion.12), channel_id=2, replica_groups=mesh['y'=4,'z'=4,'core'=2,'batch'=4] {'y','z'}, dimensions={0}, use_global_device_ids=true | all-gather | bytes 5013504 | tf_op jit(solution)/shard_map/all_gather | solution.py:283
  125.3 2.1 %copy-done.7 = f16[2304,1024]{1,0:T(8,128)(2,1)} copy-done((f16[2304,1024]{1,0:T(8,128)(2,1)}, f16[2304,1024]{1,0:T(8,128)(2,1)S(1)}, u32[]{:S(2)}) %copy-start.7) | copy-done | bytes 4718616
  131.6 2.1 %convert_reduce_fusion = (f32[1024]{0:T(1024)S(1)}, bf16[2304,1024]{1,0:T(8,128)(2,1)S(1)}) fusion(f32[2304]{0:T(1024)S(1)} %fusion.4, f16[2304,1024]{1,0:T(8,128)(2,1)S(1)} %bitcast.87, bf16[2304,8]{1,0:T(8,128)(2,1)S(1)} %get-tuple-element.31, bf16[1024,8]{0,1:T(8,128)(2,1)S(1)} %copy-done), kind=kOutput, calls=%fused_computation.3 | convolution fusion | flops 51903488 | bytes 9503744 | tf_op jit(solution)/shard_map/dot_general | solution.py:306
  133.6 2.0 %fusion.2 = f32[384,1024]{1,0:T(8,128)S(1)} fusion(bf16[2304,1024]{1,0:T(8,128)(2,1)S(1)} %get-tuple-element.58, bf16[2304,512]{1,0:T(8,128)(2,1)S(1)} %bitcast.81), kind=kOutput, calls=%fused_computation.5 | convolution fusion | flops 1811939328 | bytes 8060928 | tf_op jit(solution)/shard_map/dot_general | solution.py:318
  138.3 12.4 %all_to_all.16 = f32[32,1,640]{2,1,0:T(1,128)S(1)} all-to-all(f32[32,1,640]{2,1,0:T(1,128)S(1)} %broadcast_in_dim.5), channel_id=1, replica_groups=mesh['y'=4,'z'=4,'core'=2,'batch'=4] {'y','z','core'}, dimensions={0} | all-to-all | bytes 163840 | tf_op jit(solution)/shard_map/all_to_all | solution.py:169
  151.2 2.0 %collective-permute-start.6 = (f32[16,640]{1,0:T(8,128)S(1)}, f32[16,640]{1,0:T(8,128)S(1)}, u32[]{:S(2)}, u32[]{:S(2)}) collective-permute-start(f32[16,640]{1,0:T(8,128)S(1)} %reduce_sum.39), channel_id=1, source_target_pairs={{0,1},{1,2},{2,3},{3,0},{4,5},{5,6},{6,7},{7,4},{8,9},{9,10},{10,1... | collective-permute-start | bytes 122888 | tf_op jit(solution)/shard_map/ppermute | solution.py:174
  153.2 3.0 %collective-permute-start.7 = (f32[16,640]{1,0:T(8,128)S(1)}, f32[16,640]{1,0:T(8,128)S(1)}, u32[]{:S(2)}, u32[]{:S(2)}) collective-permute-start(f32[16,640]{1,0:T(8,128)S(1)} %reduce_sum.39), channel_id=1, source_target_pairs={{0,2},{1,3},{2,0},{3,1},{4,6},{5,7},{6,4},{7,5},{8,10},{9,11},{10,... | collective-permute-start | bytes 122888 | tf_op jit(solution)/shard_map/ppermute | solution.py:174
  156.7 2.0 %collective-permute-done.7 = f32[16,640]{1,0:T(8,128)S(1)} collective-permute-done((f32[16,640]{1,0:T(8,128)S(1)}, f32[16,640]{1,0:T(8,128)S(1)}, u32[]{:S(2)}, u32[]{:S(2)}) %collective-permute-start.7) | collective-permute-done | bytes 40992 | tf_op jit(solution)/shard_map/ppermute | solution.py:174
  159.0 1.6 collective-permute-start.4
  163.0 1.5 collective-permute-start.2
  164.5 1.5 collective-permute-done.4
  166.1 3.3 %collective-permute-done.2 = f32[2,48,512]{2,1,0:T(8,128)S(1)} collective-permute-done((f32[2,48,512]{2,1,0:T(8,128)S(1)}, f32[2,48,512]{2,1,0:T(8,128)S(1)}, u32[]{:S(2)}, u32[]{:S(2)}) %collective-permute-start.2) | collective-permute-done | bytes 196640 | tf_op jit(solution)/shard_map/ppermute | solution.py:196
  169.4 1.7 collective-permute-start.3
  171.1 4.2 %collective-permute-done.3 = f32[48,512]{1,0:T(8,128)S(1)} collective-permute-done((f32[48,512]{1,0:T(8,128)S(1)}, f32[48,512]{1,0:T(8,128)S(1)}, u32[]{:S(2)}, u32[]{:S(2)}) %collective-permute-start.3) | collective-permute-done | bytes 98336 | tf_op jit(solution)/shard_map/ppermute | solution.py:196
  (98 shorter events, 18.7 us)
Async XLA Ops:
  0.6 22.0 %copy-start = (bf16[1024,8]{0,1:T(8,128)(2,1)S(1)}, bf16[1024,8]{0,1:T(8,128)(2,1)}, u32[]{:S(2)}) copy-start(bf16[1024,8]{0,1:T(8,128)(2,1)} %param.16) | copy-start | bytes 49156
  0.6 1.2 copy-start.1
  4.5 8.6 %copy-start.2 = (bf16[1,128,4096]{2,1,0:T(8,128)(2,1)S(1)}, bf16[1,128,4096]{2,1,0:T(8,128)(2,1)}, u32[]{:S(2)}) copy-start(bf16[1,128,4096]{2,1,0:T(8,128)(2,1)} %param.9) | copy-start | bytes 3145732
  4.5 8.6 %copy-start.4 = (bf16[1,128,1024]{2,1,0:T(8,128)(2,1)S(1)}, bf16[1,128,1024]{2,1,0:T(8,128)(2,1)}, u32[]{:S(2)}) copy-start(bf16[1,128,1024]{2,1,0:T(8,128)(2,1)} %param.10) | copy-start | bytes 786436
  4.5 8.6 %copy-start.10 = (f32[1024]{0:T(1024)S(1)}, f32[1024]{0:T(1024)}, u32[]{:S(2)}) copy-start(f32[1024]{0:T(1024)} %param.15) | copy-start | bytes 12292
  4.5 37.5 %all-to-all-start = ((bf16[32,2,128,128]{3,2,1,0:T(8,128)(2,1)}), bf16[32,2,128,128]{3,2,1,0:T(8,128)(2,1)S(1)}, u32[]{:S(2)}, u32[]{:S(2)}) async-start(bf16[32,2,128,128]{3,2,1,0:T(8,128)(2,1)} %by_head.1), calls=%async_computation | async-start | bytes 4194304 | tf_op jit(solution)/shard_map/all_to_all | solution.py:169
  13.1 9.5 %copy-start.11 = (f32[8]{0:T(128)S(1)}, f32[8]{0:T(128)}, u32[]{:S(2)}) copy-start(f32[8]{0:T(128)} %param.17) | copy-start | bytes 100
  27.0 2.6 %copy-start.5 = (s32[1,32]{1,0:T(1,128)S(1)}, s32[1,32]{1,0:T(1,128)}, u32[]{:S(2)}) copy-start(s32[1,32]{1,0:T(1,128)} %param.13) | copy-start | bytes 388
  27.0 3.7 %copy-start.8 = (bf16[128,16,64]{2,0,1:T(8,128)(2,1)S(1)}, bf16[128,16,64]{2,0,1:T(8,128)(2,1)}, u32[]{:S(2)}) copy-start(bf16[128,16,64]{2,0,1:T(8,128)(2,1)} %copy.45) | copy-start | bytes 786436
  62.1 4.1 %collective-permute-start = (f32[16,128]{1,0:T(8,128)S(1)}, f32[16,128]{1,0:T(8,128)S(1)}, u32[]{:S(2)}, u32[]{:S(2)}) collective-permute-start(f32[16,128]{1,0:T(8,128)S(1)} %bitcast.95), channel_id=1, source_target_pairs={{0,4},{4,0},{1,5},{5,1},{2,6},{6,2},{3,7},{7,3},{8,12},{12,8},{9,1... | collective-permute-start | bytes 24584 | tf_op jit(solution)/shard_map/ppermute | solution.py:174
  62.3 4.0 %copy-start.9 = (f16[128,1024]{1,0:T(8,128)(2,1)S(1)}, f16[128,1024]{1,0:T(8,128)(2,1)}, u32[]{:S(2)}) copy-start(f16[128,1024]{1,0:T(8,128)(2,1)} %get-tuple-element.8) | copy-start | bytes 786436
  62.3 65.9 %all-to-all-start.1 = ((bf16[16,128,512]{2,1,0:T(8,128)(2,1)}), bf16[16,128,512]{2,1,0:T(8,128)(2,1)S(1)}, u32[]{:S(2)}, u32[]{:S(2)}) async-start(bf16[16,128,512]{2,1,0:T(8,128)(2,1)} %maximum_bitcast_fusion), calls=%async_computation.1 | async-start | bytes 4194304 | tf_op jit(solution)/shard_map/all_to_all | solution.py:169
  125.3 2.1 %copy-start.7 = (f16[2304,1024]{1,0:T(8,128)(2,1)}, f16[2304,1024]{1,0:T(8,128)(2,1)S(1)}, u32[]{:S(2)}) copy-start(f16[2304,1024]{1,0:T(8,128)(2,1)S(1)} %all-gather.2) | copy-start | bytes 14155780
  128.4 5.2 %copy-start.6 = (bf16[16,144,512]{2,1,0:T(8,128)(2,1)}, bf16[16,144,512]{2,1,0:T(8,128)(2,1)S(1)}, u32[]{:S(2)}) copy-start(bf16[16,144,512]{2,1,0:T(8,128)(2,1)S(1)} %pad.26) | copy-start | bytes 7077892
  128.4 3.0 %slice-start = ((s8[4718592]{0:T(1024)(128)(4,1)}), s8[4194304]{0:T(1024)(128)(4,1)S(1)}, s32[]{:S(2)}) async-start(s8[4718592]{0:T(1024)(128)(4,1)} %bitcast.86), calls=%async_computation.3 | async-start | bytes 8388608
  128.9 2.7 %slice-start.1 = ((s8[4718592]{0:T(1024)(128)(4,1)}), s8[524288]{0:T(1024)(128)(4,1)S(1)}, s32[]{:S(2)}) async-start(s8[4718592]{0:T(1024)(128)(4,1)} %bitcast.86), calls=%async_computation.4 | async-start | bytes 1048576
  136.6 22.1 %collective-permute-start.1 = (f32[192,1024]{1,0:T(8,128)}, f32[192,1024]{1,0:T(8,128)S(1)}, u32[]{:S(2)}, u32[]{:S(2)}) collective-permute-start(f32[192,1024]{1,0:T(8,128)} %dynamic-slice_bitcast_fusion), channel_id=1, source_target_pairs={{0,4},{4,0},{1,5},{5,1},{2,6},{6,2},{3,7},{7,3},{8,12},{12,8},{9,1... | collective-permute-start | bytes 2359304 | tf_op jit(solution)/shard_map/ppermute | solution.py:174
  151.1 5.1 %collective-permute-start.8 = (f32[16,640]{1,0:T(8,128)S(1)}, f32[16,640]{1,0:T(8,128)S(1)}, u32[]{:S(2)}, u32[]{:S(2)}) collective-permute-start(f32[16,640]{1,0:T(8,128)S(1)} %reduce_sum.39), channel_id=1, source_target_pairs={{0,3},{1,0},{2,1},{3,2},{4,7},{5,4},{6,5},{7,6},{8,11},{9,8},{10,9... | collective-permute-start | bytes 122888 | tf_op jit(solution)/shard_map/ppermute | solution.py:174
  151.2 5.5 %collective-permute-start.6 = (f32[16,640]{1,0:T(8,128)S(1)}, f32[16,640]{1,0:T(8,128)S(1)}, u32[]{:S(2)}, u32[]{:S(2)}) collective-permute-start(f32[16,640]{1,0:T(8,128)S(1)} %reduce_sum.39), channel_id=1, source_target_pairs={{0,1},{1,2},{2,3},{3,0},{4,5},{5,6},{6,7},{7,4},{8,9},{9,10},{10,1... | collective-permute-start | bytes 122888 | tf_op jit(solution)/shard_map/ppermute | solution.py:174
  153.2 5.5 %collective-permute-start.7 = (f32[16,640]{1,0:T(8,128)S(1)}, f32[16,640]{1,0:T(8,128)S(1)}, u32[]{:S(2)}, u32[]{:S(2)}) collective-permute-start(f32[16,640]{1,0:T(8,128)S(1)} %reduce_sum.39), channel_id=1, source_target_pairs={{0,2},{1,3},{2,0},{3,1},{4,6},{5,7},{6,4},{7,5},{8,10},{9,11},{10,... | collective-permute-start | bytes 122888 | tf_op jit(solution)/shard_map/ppermute | solution.py:174
  159.0 7.0 %collective-permute-start.4 = (f32[2,48,512]{2,1,0:T(8,128)S(1)}, f32[2,48,512]{2,1,0:T(8,128)S(1)}, u32[]{:S(2)}, u32[]{:S(2)}) collective-permute-start(f32[2,48,512]{2,1,0:T(8,128)S(1)} %pad_maximum_fusion.2), channel_id=1, source_target_pairs={{0,3},{1,2},{2,1},{3,0},{4,7},{5,6},{6,5},{7,4},{8,11},{9,10},{10,... | collective-permute-start | bytes 589832 | tf_op jit(solution)/shard_map/ppermute | solution.py:196
  163.0 6.3 %collective-permute-start.2 = (f32[2,48,512]{2,1,0:T(8,128)S(1)}, f32[2,48,512]{2,1,0:T(8,128)S(1)}, u32[]{:S(2)}, u32[]{:S(2)}) collective-permute-start(f32[2,48,512]{2,1,0:T(8,128)S(1)} %pad_maximum_fusion.1), channel_id=1, source_target_pairs={{0,1},{1,0},{2,3},{3,2},{4,5},{5,4},{6,7},{7,6},{8,9},{9,8},{10,11... | collective-permute-start | bytes 589832 | tf_op jit(solution)/shard_map/ppermute | solution.py:196
  166.0 5.1 %collective-permute-start.5 = (f32[48,512]{1,0:T(8,128)S(1)}, f32[48,512]{1,0:T(8,128)S(1)}, u32[]{:S(2)}, u32[]{:S(2)}) collective-permute-start(f32[48,512]{1,0:T(8,128)S(1)} %slice_bitcast_fusion), channel_id=1, source_target_pairs={{0,1},{1,0},{2,3},{3,2},{4,5},{5,4},{6,7},{7,6},{8,9},{9,8},{10,11... | collective-permute-start | bytes 294920 | tf_op jit(solution)/shard_map/ppermute | solution.py:196
  169.4 5.9 %collective-permute-start.3 = (f32[48,512]{1,0:T(8,128)S(1)}, f32[48,512]{1,0:T(8,128)S(1)}, u32[]{:S(2)}, u32[]{:S(2)}) collective-permute-start(f32[48,512]{1,0:T(8,128)S(1)} %slice_bitcast_fusion.2), channel_id=1, source_target_pairs={{0,3},{1,2},{2,1},{3,0},{4,7},{5,6},{6,5},{7,4},{8,11},{9,10},{10,... | collective-permute-start | bytes 294920 | tf_op jit(solution)/shard_map/ppermute | solution.py:196
  (1 other events, 0.9 us)

commit v6 on v5

--- a/solution.py
+++ b/solution.py
@@ -14,7 +14,7 @@
 KEYS = 512
 
 
-def mass_kernel(order_ref, limit_ref, both_ref, out_ref, where_ref, keys, even, odd, col, *, scale):
+def mass_kernel(order_ref, limit_ref, core_ref, both_ref, other_ref, out_ref, where_ref, keys, even, odd, col, *, scale):
     blocks = both_ref.shape[0]
     limit = limit_ref[0]
     factor = scale * math.log2(math.e)
@@ -24,7 +24,11 @@
     def by_position(i, carry):
         p = order_ref[i]
         where_ref[p] = i
-        keys[pl.ds(pl.multiple_of(p * BLOCK, BLOCK), BLOCK), :] = both_ref[i, 1]
+        part = other_ref.shape[1]
+        mine = pl.multiple_of(p * BLOCK + core_ref[0] * part, part)
+        theirs = pl.multiple_of(p * BLOCK + (1 - core_ref[0]) * part, part)
+        keys[pl.ds(mine, part), :] = both_ref[i, BLOCK:]
+        keys[pl.ds(theirs, part), :] = other_ref[i]
         return carry
 
     lax.fori_loop(0, blocks, by_position, 0)
@@ -60,7 +64,7 @@
         return jnp.where(live & (total > 0.0), 1.0 / total, 0.0)
 
     def query_block(r, top, scores, earlier):
-        parts = [both_ref[where_ref[r * lanes + i], 0] for i in range(lanes)]
+        parts = [both_ref[where_ref[r * lanes + i], :BLOCK] for i in range(lanes)]
         q_rows = jnp.concatenate(parts, axis=0)
 
         def product(c):
@@ -112,15 +116,15 @@
     lax.fori_loop(0, blocks, store, 0)
 
 
-def head_mass(order, limit, both, scale):
-    blocks, _, rows, size = both.shape
-    tokens = blocks * rows
+def head_mass(order, limit, core, both, other, scale):
+    blocks, _, size = both.shape
+    tokens = blocks * BLOCK
     smem = pl.BlockSpec(memory_space=pltpu.SMEM)
     vmem = pl.BlockSpec(memory_space=pltpu.VMEM)
     return pl.pallas_call(
         functools.partial(mass_kernel, scale=scale),
         out_shape=jax.ShapeDtypeStruct((blocks, BLOCK), jnp.float32),
-        in_specs=[smem, smem, vmem],
+        in_specs=[smem, smem, smem, vmem, vmem],
         out_specs=vmem,
         scratch_shapes=[
             pltpu.SMEM((blocks,), jnp.int32),
@@ -134,16 +138,17 @@
             flops=2 * tokens * tokens * size, bytes_accessed=4 * tokens * size, transcendentals=tokens * tokens // 2
         ),
         name="head_mass",
-    )(order, limit, both)
+    )(order, limit, core, both, other)
 
 
 def by_head_kernel(q_ref, k_ref, out_ref):
-    heads, _, _, size = out_ref.shape
+    heads, _, size = out_ref.shape
+    rows = q_ref.shape[0]
     group = q_ref.shape[1] // k_ref.shape[1]
     for h in range(heads):
-        g = h // group
-        out_ref[h, 0] = q_ref[:, h * size : (h + 1) * size]
-        out_ref[h, 1] = k_ref[:, g * size : (g + 1) * size]
+        g, c = h // group, h % 2
+        out_ref[h, :rows] = q_ref[:, h * size : (h + 1) * size]
+        out_ref[h, rows:] = k_ref[c * rows // 2 : (c + 1) * rows // 2, g * size : (g + 1) * size]
 
 
 def by_head(q_rows, k_rows, size):
@@ -151,7 +156,7 @@
     vmem = pl.BlockSpec(memory_space=pltpu.VMEM)
     return pl.pallas_call(
         by_head_kernel,
-        out_shape=jax.ShapeDtypeStruct((width // size, 2, rows, size), q_rows.dtype),
+        out_shape=jax.ShapeDtypeStruct((width // size, rows + rows // 2, size), q_rows.dtype),
         in_specs=[vmem, vmem],
         out_specs=vmem,
         compiler_params=pltpu.CompilerParams(vmem_limit_bytes=16 * 1024 * 1024),
@@ -266,9 +271,10 @@
         ],
         axis=2,
     )
-    both, slope, carried = lax.optimization_barrier((both, slope, jnp.moveaxis(carried, 1, 0)))
+    other = shifted(both[:, rows:], "core", 1)
+    both, other, slope, carried = lax.optimization_barrier((both, other, slope, jnp.moveaxis(carried, 1, 0)))
     spread = exchanged(carried, PLANE)
-    partial = head_mass(order, lengths, both, 1.0 / math.sqrt(head_size))
+    partial = head_mass(order, lengths, core.reshape(1).astype(jnp.int32), both, other, 1.0 / math.sqrt(head_size))
 
     by_core = partial.reshape(chips, cores, rows)
     both_heads = lax.dynamic_index_in_dim(by_core, core, 1, keepdims=False)

time: 177 us -> 179 us (1.011)
  waiting for transfers between devices: 19.4 us -> 22.2 us
    all_to_all x2, waiting for transfers between devices: 8.02 us -> 10.8 us  [exchanged(): return lax.all_to_all(array, axis, 0, 0, tiled=True)]
    ppermute x5 -> x6, starting transfers between devices: 5.19 us -> 5.7 us  [shifted(): lax.ppermute(array, axis, [(i, (i + by) % size) for i in range(size)])]
    unnamed x31 -> x29, local copies, waits for them, and re-layouts: 6.3 us -> 6.3 us
  transfers between devices with their start and end apart: 11 -> 12, of which waited for: 6 -> 6; matrix products, arithmetic and copies ran while one was open for 14% -> 14% of each run, Pallas kernels for 0% -> 0%
where the time goes in v6:
time: 179 us
  blocking collectives  70.2 us (39%)
  starting transfers between devices  22.9 us (13%)
  waiting for transfers between devices  22.2 us (12%)
  Pallas kernels  21.6 us (12%)
  local copies, waits for them, and re-layouts  15.4 us (9%)
  matrix products  13.1 us (7%)
  other arithmetic  11.5 us (6%)
    all_gather x1, blocking collectives, on_device(): lax.all_gather(jnp.concatenate([slope, carry]), PLANE, axis=0, tiled=False)  57.4 us
    pallas_call x1, Pallas kernels, head_mass(): pl.pallas_call(functools.partial(mass_kernel, scale=scale), out_shape=jax...  20.2 us
    all_to_all x1, blocking collectives, exchanged(): return lax.all_to_all(array, axis, 0, 0, tiled=True)  12.8 us
    all_to_all x2, starting transfers between devices, exchanged(): return lax.all_to_all(array, axis, 0, 0, tiled=True)  12.3 us
    all_to_all x2, waiting for transfers between devices, exchanged(): return lax.all_to_all(array, axis, 0, 0, tiled=True)  10.8 us
    ppermute x4, waiting for transfers between devices, swapped(): return lax.ppermute(array, 'batch', [(i, other(i)) for i in range(SIDE)])  8.91 us
    dot_general x1, matrix products, on_device(): pre = jnp.dot(features, w_in, preferred_element_type=jnp.float32) + b_in  6.58 us
    unnamed x29, local copies, waits for them, and re-layouts  6.3 us
  transfers between devices with their start and end apart: 12, of which 6 were waited for; matrix products, arithmetic and copies ran while one was open for 14% of the time, Pallas kernels for 0%

profile of v6, /device:TPU:0, one launch (start us, length us, event | category | flops | bytes accessed | tf_op | source)
XLA Modules:
  0.0 178.8 jit_solution(3129759715015273004)
XLA Ops:
  2.8 1.4 by_head.1
  4.2 8.6 %all-to-all-start = ((bf16[32,192,128]{2,1,0:T(8,128)(2,1)}), bf16[32,192,128]{2,1,0:T(8,128)(2,1)S(1)}, u32[]{:S(2)}, u32[]{:S(2)}) async-start(bf16[32,192,128]{2,1,0:T(8,128)(2,1)} %by_head.1), calls=%async_computation | async-start | bytes 3145728 | tf_op jit(solution)/shard_map/all_to_all | solution.py:174
  12.9 6.6 %abs_reduce_fusion = (f32[128]{0:T(128)S(1)}, f32[128,1024]{1,0:T(8,128)S(1)}) fusion(f32[1024]{0:T(1024)S(1)} %copy-done.9, bf16[6144,1024]{1,0:T(8,128)(2,1)} %param.14, bf16[128,1024]{1,0:T(8,128)(2,1)S(1)} %bitcast.94, bf16[128,1024]{1,0:T(8,128)(2,1)S(1)} %bitcast.76, bf16[128,4096]{1,0:T(8,128)(2,1)S(1)} %bitcast.73), kind=kOutput, calls=%fused_computation.32 | convolution fusion | flops 1616641920 | bytes 14684672 | tf_op jit(solution)/shard_map/dot_general | solution.py:251
  22.7 2.3 %pad_maximum_fusion = bf16[128,6144]{1,0:T(8,128)(2,1)} fusion(bf16[128,1024]{1,0:T(8,128)(2,1)} %bitcast.93, bf16[128,1024]{1,0:T(8,128)(2,1)S(1)} %bitcast.77, bf16[128,4096]{1,0:T(8,128)(2,1)S(1)} %bitcast.74), kind=kLoop, calls=%fused_computation.8 | loop fusion | flops 4718592 | bytes 3145728 | tf_op jit(solution)/shard_map/concatenate | solution.py:250
  25.0 10.8 %all-to-all-done.both_ref = bf16[32,192,128]{2,1,0:T(8,128)(2,1)S(1)} async-done(((bf16[32,192,128]{2,1,0:T(8,128)(2,1)}), bf16[32,192,128]{2,1,0:T(8,128)(2,1)S(1)}, u32[]{:S(2)}, u32[]{:S(2)}) %all-to-all-start) | async-done | bytes 1572896 | tf_op jit(solution)/shard_map/all_to_all | solution.py:174
  37.2 2.8 %copy.56 = bf16[16,16,8,384]{3,2,0,1:T(8,128)(2,1)} copy(bf16[16,16,8,384]{3,2,1,0:T(8,128)(2,1)} %bitcast.84) | data formatting | bytes 3145728 | tf_op jit(solution)/shard_map/reshape | solution.py:263
  42.2 3.2 %maximum_bitcast_fusion = bf16[16,128,512]{2,1,0:T(8,128)(2,1)} fusion(bf16[128,16,64]{2,0,1:T(8,128)(2,1)S(1)} %broadcast_in_dim.4, bf16[128,16,64]{2,0,1:T(8,128)(2,1)S(1)} %copy.45, bf16[128,16,384]{2,0,1:T(8,128)(2,1)} %bitcast.85), kind=kLoop, calls=%fused_computation.4 | loop fusion | flops 6291456 | bytes 4194304 | tf_op jit(solution)/shard_map/transpose | solution.py:275
  45.5 20.2 %head_mass.1 = f32[32,128]{1,0:T(8,128)S(1)} custom-call(s32[32]{0:T(128)S(1)} %bitcast.79, s32[1]{0:T(128)} %copy.57.limit_ref, s32[1]{0:T(128)} %bitcast.8.core_ref, bf16[32,192,128]{2,1,0:T(8,128)(2,1)S(1)} %all-to-all-done.both_ref, bf16[32,64,128]{2,1,0:T(8,128)(2,1)S(1)} %collective-permute-done.other_ref), custom_call_target="tpu_custom_call" | custom-call | flops 4294967296 | bytes 2097152 | tf_op jit(solution)/shard_map/head_mass/pallas_call | solution.py:124
  66.4 3.7 %all-to-all-start.1 = ((bf16[16,128,512]{2,1,0:T(8,128)(2,1)}), bf16[16,128,512]{2,1,0:T(8,128)(2,1)S(1)}, u32[]{:S(2)}, u32[]{:S(2)}) async-start(bf16[16,128,512]{2,1,0:T(8,128)(2,1)} %maximum_bitcast_fusion), calls=%async_computation.1 | async-start | bytes 4194304 | tf_op jit(solution)/shard_map/all_to_all | solution.py:174
  70.3 57.4 %all-gather.2 = f16[2304,1024]{1,0:T(8,128)(2,1)S(1)} all-gather(f16[144,1024]{1,0:T(8,128)(2,1)S(1)} %fusion.12), channel_id=2, replica_groups=mesh['y'=4,'z'=4,'core'=2,'batch'=4] {'y','z'}, dimensions={0}, use_global_device_ids=true | all-gather | bytes 5013504 | tf_op jit(solution)/shard_map/all_gather | solution.py:289
  127.7 2.1 %copy-done.7 = f16[2304,1024]{1,0:T(8,128)(2,1)} copy-done((f16[2304,1024]{1,0:T(8,128)(2,1)}, f16[2304,1024]{1,0:T(8,128)(2,1)S(1)}, u32[]{:S(2)}) %copy-start.7) | copy-done | bytes 4718616
  133.9 2.1 %convert_reduce_fusion = (f32[1024]{0:T(1024)S(1)}, bf16[2304,1024]{1,0:T(8,128)(2,1)S(1)}) fusion(f32[2304]{0:T(1024)S(1)} %fusion.4, f16[2304,1024]{1,0:T(8,128)(2,1)S(1)} %bitcast.88, bf16[2304,8]{1,0:T(8,128)(2,1)S(1)} %get-tuple-element.33, bf16[1024,8]{0,1:T(8,128)(2,1)S(1)} %copy-done), kind=kOutput, calls=%fused_computation.3 | convolution fusion | flops 51903488 | bytes 9503744 | tf_op jit(solution)/shard_map/dot_general | solution.py:312
  136.0 2.0 %fusion.2 = f32[384,1024]{1,0:T(8,128)S(1)} fusion(bf16[2304,1024]{1,0:T(8,128)(2,1)S(1)} %get-tuple-element.60, bf16[2304,512]{1,0:T(8,128)(2,1)S(1)} %bitcast.82), kind=kOutput, calls=%fused_computation.5 | convolution fusion | flops 1811939328 | bytes 8060928 | tf_op jit(solution)/shard_map/dot_general | solution.py:324
  139.1 1.4 fusion.9
  140.7 12.8 %all_to_all.16 = f32[32,1,640]{2,1,0:T(1,128)S(1)} all-to-all(f32[32,1,640]{2,1,0:T(1,128)S(1)} %broadcast_in_dim.5), channel_id=1, replica_groups=mesh['y'=4,'z'=4,'core'=2,'batch'=4] {'y','z','core'}, dimensions={0} | all-to-all | bytes 163840 | tf_op jit(solution)/shard_map/all_to_all | solution.py:174
  153.9 2.0 %collective-permute-start.7 = (f32[16,640]{1,0:T(8,128)S(1)}, f32[16,640]{1,0:T(8,128)S(1)}, u32[]{:S(2)}, u32[]{:S(2)}) collective-permute-start(f32[16,640]{1,0:T(8,128)S(1)} %reduce_sum.39), channel_id=1, source_target_pairs={{0,1},{1,2},{2,3},{3,0},{4,5},{5,6},{6,7},{7,4},{8,9},{9,10},{10,1... | collective-permute-start | bytes 122888 | tf_op jit(solution)/shard_map/ppermute | solution.py:179
  156.0 3.0 %collective-permute-start.8 = (f32[16,640]{1,0:T(8,128)S(1)}, f32[16,640]{1,0:T(8,128)S(1)}, u32[]{:S(2)}, u32[]{:S(2)}) collective-permute-start(f32[16,640]{1,0:T(8,128)S(1)} %reduce_sum.39), channel_id=1, source_target_pairs={{0,2},{1,3},{2,0},{3,1},{4,6},{5,7},{6,4},{7,5},{8,10},{9,11},{10,... | collective-permute-start | bytes 122888 | tf_op jit(solution)/shard_map/ppermute | solution.py:179
  159.5 2.0 %collective-permute-done.8 = f32[16,640]{1,0:T(8,128)S(1)} collective-permute-done((f32[16,640]{1,0:T(8,128)S(1)}, f32[16,640]{1,0:T(8,128)S(1)}, u32[]{:S(2)}, u32[]{:S(2)}) %collective-permute-start.8) | collective-permute-done | bytes 40992 | tf_op jit(solution)/shard_map/ppermute | solution.py:179
  161.8 1.6 collective-permute-start.5
  165.8 1.5 collective-permute-start.3
  167.3 1.4 collective-permute-done.5
  168.9 3.3 %collective-permute-done.3 = f32[2,48,512]{2,1,0:T(8,128)S(1)} collective-permute-done((f32[2,48,512]{2,1,0:T(8,128)S(1)}, f32[2,48,512]{2,1,0:T(8,128)S(1)}, u32[]{:S(2)}, u32[]{:S(2)}) %collective-permute-start.3) | collective-permute-done | bytes 196640 | tf_op jit(solution)/shard_map/ppermute | solution.py:201
  172.2 1.7 collective-permute-start.4
  173.9 4.2 %collective-permute-done.4 = f32[48,512]{1,0:T(8,128)S(1)} collective-permute-done((f32[48,512]{1,0:T(8,128)S(1)}, f32[48,512]{1,0:T(8,128)S(1)}, u32[]{:S(2)}, u32[]{:S(2)}) %collective-permute-start.4) | collective-permute-done | bytes 98336 | tf_op jit(solution)/shard_map/ppermute | solution.py:201
  (99 shorter events, 18.9 us)
Async XLA Ops:
  0.6 20.9 %copy-start = (bf16[1024,8]{0,1:T(8,128)(2,1)S(1)}, bf16[1024,8]{0,1:T(8,128)(2,1)}, u32[]{:S(2)}) copy-start(bf16[1024,8]{0,1:T(8,128)(2,1)} %param.16) | copy-start | bytes 49156
  0.6 1.2 copy-start.1
  4.2 8.6 %copy-start.2 = (bf16[1,128,4096]{2,1,0:T(8,128)(2,1)S(1)}, bf16[1,128,4096]{2,1,0:T(8,128)(2,1)}, u32[]{:S(2)}) copy-start(bf16[1,128,4096]{2,1,0:T(8,128)(2,1)} %param.9) | copy-start | bytes 3145732
  4.2 8.6 %copy-start.4 = (bf16[1,128,1024]{2,1,0:T(8,128)(2,1)S(1)}, bf16[1,128,1024]{2,1,0:T(8,128)(2,1)}, u32[]{:S(2)}) copy-start(bf16[1,128,1024]{2,1,0:T(8,128)(2,1)} %param.10) | copy-start | bytes 786436
  4.2 8.6 %copy-start.8 = (bf16[1,128,1024]{2,1,0:T(8,128)(2,1)S(1)}, bf16[1,128,1024]{2,1,0:T(8,128)(2,1)}, u32[]{:S(2)}) copy-start(bf16[1,128,1024]{2,1,0:T(8,128)(2,1)} %param.11) | copy-start | bytes 786436
  4.2 8.6 %copy-start.9 = (f32[1024]{0:T(1024)S(1)}, f32[1024]{0:T(1024)}, u32[]{:S(2)}) copy-start(f32[1024]{0:T(1024)} %param.15) | copy-start | bytes 12292
  4.2 31.6 %all-to-all-start = ((bf16[32,192,128]{2,1,0:T(8,128)(2,1)}), bf16[32,192,128]{2,1,0:T(8,128)(2,1)S(1)}, u32[]{:S(2)}, u32[]{:S(2)}) async-start(bf16[32,192,128]{2,1,0:T(8,128)(2,1)} %by_head.1), calls=%async_computation | async-start | bytes 3145728 | tf_op jit(solution)/shard_map/all_to_all | solution.py:174
  12.9 8.7 %copy-start.10 = (f32[8]{0:T(128)S(1)}, f32[8]{0:T(128)}, u32[]{:S(2)}) copy-start(f32[8]{0:T(128)} %param.17) | copy-start | bytes 100
  36.6 4.5 %copy-start.5 = (s32[1,32]{1,0:T(1,128)S(1)}, s32[1,32]{1,0:T(1,128)}, u32[]{:S(2)}) copy-start(s32[1,32]{1,0:T(1,128)} %param.13) | copy-start | bytes 388
  36.7 8.8 %collective-permute-start = (bf16[32,64,128]{2,1,0:T(8,128)(2,1)}, bf16[32,64,128]{2,1,0:T(8,128)(2,1)S(1)}, u32[]{:S(2)}, u32[]{:S(2)}) collective-permute-start(bf16[32,64,128]{2,1,0:T(8,128)(2,1)} %slice.96), channel_id=1, source_target_pairs={{0,4},{4,0},{1,5},{5,1},{2,6},{6,2},{3,7},{7,3},{8,12},{12,8},{9,1... | collective-permute-start | bytes 1572872 | tf_op jit(solution)/shard_map/ppermute | solution.py:179
  65.7 4.4 %collective-permute-start.1 = (f32[16,128]{1,0:T(8,128)S(1)}, f32[16,128]{1,0:T(8,128)S(1)}, u32[]{:S(2)}, u32[]{:S(2)}) collective-permute-start(f32[16,128]{1,0:T(8,128)S(1)} %bitcast.96), channel_id=1, source_target_pairs={{0,4},{4,0},{1,5},{5,1},{2,6},{6,2},{3,7},{7,3},{8,12},{12,8},{9,1... | collective-permute-start | bytes 24584 | tf_op jit(solution)/shard_map/ppermute | solution.py:179
  66.4 64.2 %all-to-all-start.1 = ((bf16[16,128,512]{2,1,0:T(8,128)(2,1)}), bf16[16,128,512]{2,1,0:T(8,128)(2,1)S(1)}, u32[]{:S(2)}, u32[]{:S(2)}) async-start(bf16[16,128,512]{2,1,0:T(8,128)(2,1)} %maximum_bitcast_fusion), calls=%async_computation.1 | async-start | bytes 4194304 | tf_op jit(solution)/shard_map/all_to_all | solution.py:174
  127.7 2.1 %copy-start.7 = (f16[2304,1024]{1,0:T(8,128)(2,1)}, f16[2304,1024]{1,0:T(8,128)(2,1)S(1)}, u32[]{:S(2)}) copy-start(f16[2304,1024]{1,0:T(8,128)(2,1)S(1)} %all-gather.2) | copy-start | bytes 14155780
  130.8 5.2 %copy-start.6 = (bf16[16,144,512]{2,1,0:T(8,128)(2,1)}, bf16[16,144,512]{2,1,0:T(8,128)(2,1)S(1)}, u32[]{:S(2)}) copy-start(bf16[16,144,512]{2,1,0:T(8,128)(2,1)S(1)} %pad.26) | copy-start | bytes 7077892
  130.8 3.0 %slice-start = ((s8[4718592]{0:T(1024)(128)(4,1)}), s8[4194304]{0:T(1024)(128)(4,1)S(1)}, s32[]{:S(2)}) async-start(s8[4718592]{0:T(1024)(128)(4,1)} %bitcast.87), calls=%async_computation.3 | async-start | bytes 8388608
  131.3 2.7 %slice-start.1 = ((s8[4718592]{0:T(1024)(128)(4,1)}), s8[524288]{0:T(1024)(128)(4,1)S(1)}, s32[]{:S(2)}) async-start(s8[4718592]{0:T(1024)(128)(4,1)} %bitcast.87), calls=%async_computation.4 | async-start | bytes 1048576
  139.0 22.5 %collective-permute-start.2 = (f32[192,1024]{1,0:T(8,128)}, f32[192,1024]{1,0:T(8,128)S(1)}, u32[]{:S(2)}, u32[]{:S(2)}) collective-permute-start(f32[192,1024]{1,0:T(8,128)} %dynamic-slice_bitcast_fusion), channel_id=1, source_target_pairs={{0,4},{4,0},{1,5},{5,1},{2,6},{6,2},{3,7},{7,3},{8,12},{12,8},{9,1... | collective-permute-start | bytes 2359304 | tf_op jit(solution)/shard_map/ppermute | solution.py:179
  153.9 5.1 %collective-permute-start.9 = (f32[16,640]{1,0:T(8,128)S(1)}, f32[16,640]{1,0:T(8,128)S(1)}, u32[]{:S(2)}, u32[]{:S(2)}) collective-permute-start(f32[16,640]{1,0:T(8,128)S(1)} %reduce_sum.39), channel_id=1, source_target_pairs={{0,3},{1,0},{2,1},{3,2},{4,7},{5,4},{6,5},{7,6},{8,11},{9,8},{10,9... | collective-permute-start | bytes 122888 | tf_op jit(solution)/shard_map/ppermute | solution.py:179
  153.9 5.6 %collective-permute-start.7 = (f32[16,640]{1,0:T(8,128)S(1)}, f32[16,640]{1,0:T(8,128)S(1)}, u32[]{:S(2)}, u32[]{:S(2)}) collective-permute-start(f32[16,640]{1,0:T(8,128)S(1)} %reduce_sum.39), channel_id=1, source_target_pairs={{0,1},{1,2},{2,3},{3,0},{4,5},{5,6},{6,7},{7,4},{8,9},{9,10},{10,1... | collective-permute-start | bytes 122888 | tf_op jit(solution)/shard_map/ppermute | solution.py:179
  156.0 5.5 %collective-permute-start.8 = (f32[16,640]{1,0:T(8,128)S(1)}, f32[16,640]{1,0:T(8,128)S(1)}, u32[]{:S(2)}, u32[]{:S(2)}) collective-permute-start(f32[16,640]{1,0:T(8,128)S(1)} %reduce_sum.39), channel_id=1, source_target_pairs={{0,2},{1,3},{2,0},{3,1},{4,6},{5,7},{6,4},{7,5},{8,10},{9,11},{10,... | collective-permute-start | bytes 122888 | tf_op jit(solution)/shard_map/ppermute | solution.py:179
  161.8 7.0 %collective-permute-start.5 = (f32[2,48,512]{2,1,0:T(8,128)S(1)}, f32[2,48,512]{2,1,0:T(8,128)S(1)}, u32[]{:S(2)}, u32[]{:S(2)}) collective-permute-start(f32[2,48,512]{2,1,0:T(8,128)S(1)} %pad_maximum_fusion.2), channel_id=1, source_target_pairs={{0,3},{1,2},{2,1},{3,0},{4,7},{5,6},{6,5},{7,4},{8,11},{9,10},{10,... | collective-permute-start | bytes 589832 | tf_op jit(solution)/shard_map/ppermute | solution.py:201
  165.8 6.3 %collective-permute-start.3 = (f32[2,48,512]{2,1,0:T(8,128)S(1)}, f32[2,48,512]{2,1,0:T(8,128)S(1)}, u32[]{:S(2)}, u32[]{:S(2)}) collective-permute-start(f32[2,48,512]{2,1,0:T(8,128)S(1)} %pad_maximum_fusion.1), channel_id=1, source_target_pairs={{0,1},{1,0},{2,3},{3,2},{4,5},{5,4},{6,7},{7,6},{8,9},{9,8},{10,11... | collective-permute-start | bytes 589832 | tf_op jit(solution)/shard_map/ppermute | solution.py:201
  168.8 5.1 %collective-permute-start.6 = (f32[48,512]{1,0:T(8,128)S(1)}, f32[48,512]{1,0:T(8,128)S(1)}, u32[]{:S(2)}, u32[]{:S(2)}) collective-permute-start(f32[48,512]{1,0:T(8,128)S(1)} %slice_bitcast_fusion), channel_id=1, source_target_pairs={{0,1},{1,0},{2,3},{3,2},{4,5},{5,4},{6,7},{7,6},{8,9},{9,8},{10,11... | collective-permute-start | bytes 294920 | tf_op jit(solution)/shard_map/ppermute | solution.py:201
  172.2 5.9 %collective-permute-start.4 = (f32[48,512]{1,0:T(8,128)S(1)}, f32[48,512]{1,0:T(8,128)S(1)}, u32[]{:S(2)}, u32[]{:S(2)}) collective-permute-start(f32[48,512]{1,0:T(8,128)S(1)} %slice_bitcast_fusion.2), channel_id=1, source_target_pairs={{0,3},{1,2},{2,1},{3,0},{4,7},{5,6},{6,5},{7,4},{8,11},{9,10},{10,... | collective-permute-start | bytes 294920 | tf_op jit(solution)/shard_map/ppermute | solution.py:201
  (1 other events, 0.9 us)
